TPU v7x, 128 devices: a whole 4x4x4 slice. The times are simulated.
128 devices in a mesh: data: 1, cols: 16 (over z, y), model: 8 (over x, core).
Axes of the slice: x: 4, y: 4, z: 4, core: 2. Of those that a mesh axis runs over, the one named last changes fastest.
Arguments:
- x_in: bfloat16 [8, 128, 128, 128], P('data', None, None, ('model', 'cols'))
- w_conv1: bfloat16 [3, 3, 128, 256], P(None, None, ('model', 'cols'))
- b_conv1: float32 [256], replicated
- w_conv2: bfloat16 [3, 3, 256, 256], replicated
- b_conv2: float32 [256], replicated
Outputs:
- output: float32 [8, 128, 128, 256], P('data', 'model', 'cols')
All inputs are finite; a program needn't handle non-finite values.
Results may differ from a plain program's by a relative error of at most 0.001.
Values are sent between devices in bfloat16 or wider.
A program may use at most 1 GiB of HBM per device.

v0:
```python
import jax
import jax.numpy as jnp
from jax import lax
from jax.sharding import PartitionSpec as P

CONV_DIMS = ("NHWC", "HWIO", "NHWC")
GROUP_AXES = ("model", "cols")


def halo_tiles(full, n_rows, n_cols):
    batch, height, width, channels = full.shape
    tile_h = height // n_rows
    tile_w = width // n_cols
    blocks = full.reshape(batch, n_rows, tile_h, width, channels)
    zero_row = jnp.zeros((batch, 1, width, channels), full.dtype)
    above = jnp.concatenate([zero_row, blocks[:, :-1, tile_h - 1]], axis=1)
    below = jnp.concatenate([blocks[:, 1:, 0], zero_row], axis=1)
    row_ext = jnp.concatenate([above[:, :, None], blocks, below[:, :, None]], axis=2)
    grid = row_ext.reshape(batch, n_rows, tile_h + 2, n_cols, tile_w, channels)
    zero_col = jnp.zeros((batch, n_rows, tile_h + 2, 1, channels), full.dtype)
    left = jnp.concatenate([zero_col, grid[:, :, :, :-1, tile_w - 1]], axis=3)
    right = jnp.concatenate([grid[:, :, :, 1:, 0], zero_col], axis=3)
    windows = jnp.concatenate([left[:, :, :, :, None], grid, right[:, :, :, :, None]], axis=4)
    windows = windows.transpose(1, 3, 0, 2, 4, 5)
    return windows.reshape(n_rows * n_cols, batch, tile_h + 2, tile_w + 2, channels)


def bias_relu(z_tile, bias, row_idx, col_idx, height, width):
    tile_h = z_tile.shape[1] - 2
    tile_w = z_tile.shape[2] - 2
    rows_at = row_idx * tile_h - 1 + jnp.arange(tile_h + 2)
    cols_at = col_idx * tile_w - 1 + jnp.arange(tile_w + 2)
    row_ok = (rows_at >= 0) & (rows_at < height)
    col_ok = (cols_at >= 0) & (cols_at < width)
    inside = row_ok[:, None, None] & col_ok[None, :, None]
    return jnp.where(inside, jnp.maximum(z_tile + bias, 0.0), 0.0).astype(jnp.bfloat16)


def solution(mesh):
    n_rows = mesh.shape["model"]
    n_cols = mesh.shape["cols"]

    def run_local(x_in, w_conv1, b_conv1, w_conv2, b_conv2):
        height = x_in.shape[1]
        width = x_in.shape[2]
        part_sum = lax.conv_general_dilated(x_in, w_conv1, (1, 1), "SAME", dimension_numbers=CONV_DIMS, preferred_element_type=jnp.float32)
        windows = halo_tiles(part_sum, n_rows, n_cols)
        z_tile = lax.psum_scatter(windows, GROUP_AXES, scatter_dimension=0, tiled=False)
        act_tile = bias_relu(z_tile, b_conv1, lax.axis_index("model"), lax.axis_index("cols"), height, width)
        out_tile = lax.conv_general_dilated(act_tile, w_conv2, (1, 1), "VALID", dimension_numbers=CONV_DIMS, preferred_element_type=jnp.float32)
        return out_tile + b_conv2

    return jax.shard_map(
        run_local,
        mesh=mesh,
        in_specs=(P("data", None, None, GROUP_AXES), P(None, None, GROUP_AXES, None), P(), P(), P()),
        out_specs=P("data", "model", "cols", None),
        check_vma=False,
    )
```

profile of v0, /device:TPU:1, one launch (start us, length us, event | category | flops | bytes accessed | tf_op | source)
XLA Modules:
  0.0 1026.9 jit_solution(7575951317404319320)
XLA Ops:
  6.5 0.0 copy-start
  6.5 0.0 reduce-scatter.2.cloned.1.call-start
  6.5 12.0 %copy.6 = bf16[8,128,128,1]{0,3,2,1:T(2,128)(2,1)} copy(bf16[8,128,128,1]{2,1,3,0:T(8,128)(2,1)} %param.5) | data formatting | bytes 524288 | tf_op args[0]
  18.5 52.9 %fusion.8 = f32[8,128,128,256]{3,0,2,1:T(8,128)} fusion(bf16[8,128,128,1]{0,3,2,1:T(2,128)(2,1)} %copy.6, bf16[3,3,1,256]{3,1,2,0:T(4,128)(2,1)} %param.6), kind=kOutput, calls=%fused_computation.17 | convolution fusion | flops 597704704 | bytes 134484480 | tf_op jit(solution)/shard_map/conv_general_dilated | solution.py:46
  71.4 11.3 %slice_bitcast_fusion.1 = (f32[8,7,128,256]{3,0,2,1:T(8,128)}, f32[8,7,128,256]{3,0,2,1:T(8,128)}) fusion(f32[8,8,16,128,256]{4,0,3,2,1:T(8,128)} %bitcast), kind=kLoop, calls=%fused_computation.8 | loop fusion | bytes 29360128 | tf_op jit(solution)/shard_map/squeeze | solution.py:16
  82.7 3.8 concatenate.25
  86.5 0.0 copy-start.1
  86.5 6.8 concatenate.28
  93.3 0.0 copy-start.2
  93.3 27.0 %maximum_bitcast_fusion.1 = (f32[8,8,18,15,256]{4,0,3,2,1:T(8,128)}, f32[8,8,18,15,256]{4,0,3,2,1:T(8,128)}) fusion(f32[8,8,1,16,8,256]{5,0,4,3,2,1:T(8,128)S(1)} %bitcast.36, f32[8,8,16,16,8,256]{5,0,4,3,2,1:T(8,128)} %bitcast.3, f32[8,8,1,16,8,256]{5,0,4,3,2,1:T(8,128)S(1)} %bitcast.34), kind=kLoop, calls=%fused_computation.6 | loop fusion | flops 17694720 | bytes 186384384 | tf_op jit(solution)/shard_map/squeeze | solution.py:21
  120.3 0.0 copy-done.1
  120.3 0.0 copy-done.2
  120.3 23.9 %pad_bitcast_fusion = (f32[8,8,18,16,1,256]{5,0,4,3,2,1:T(8,128)}, f32[8,8,18,16,1,256]{5,0,4,3,2,1:T(8,128)}) fusion(f32[8,8,18,15,256]{4,0,3,2,1:T(8,128)} %get-tuple-element.6, f32[8,8,18,15,256]{4,0,3,2,1:T(8,128)} %get-tuple-element.5), kind=kLoop, calls=%fused_computation.1 | loop fusion | bytes 73138176 | tf_op jit(solution)/shard_map/broadcast_in_dim | solution.py:23
  144.2 128.4 %maximum_bitcast_fusion = f32[8,16,8,18,10,256]{5,2,4,1,3,0:T(8,128)} fusion(f32[8,8,18,16,1,256]{5,0,4,3,2,1:T(8,128)} %get-tuple-element.9, f32[8,8,1,16,8,256]{5,0,4,3,2,1:T(8,128)} %bitcast.37, f32[8,8,16,16,8,256]{5,0,4,3,2,1:T(8,128)} %bitcast.3, f32[8,8,1,16,8,256]{5,0,4,3,2,1:T(8,128)} %bitcast.35, f32[8,8,18,16,1,256]{5,0,4,3,2,1:T(8,128)} %get-tuple-element.10), kind=kLoop, calls=%fused_computation | loop fusion | flops 188743680 | bytes 377487360 | tf_op jit(solution)/shard_map/transpose | solution.py:24
  272.6 121.5 %copy.10 = f32[8,16,8,18,10,256]{5,2,4,3,1,0:T(8,128)} copy(f32[8,16,8,18,10,256]{5,2,4,1,3,0:T(8,128)} %maximum_bitcast_fusion) | data formatting | bytes 377487360 | tf_op jit(solution)/shard_map/transpose | solution.py:24
  394.1 0.0 copy-start.3
  394.1 0.0 copy-start.4
  394.1 0.0 reduce-scatter.2.cloned.1.call-update
  394.2 0.1 broadcast_and_fusion
  394.3 621.6 %reduce-scatter.2.cloned.1.call-done = f32[1,8,18,10,256]{4,1,3,2,0:T(8,128)} async-done(((f32[128,8,18,10,256]{4,1,3,2,0:T(8,128)}), f32[1,8,18,10,256]{4,1,3,2,0:T(8,128)}) %reduce-scatter.2.cloned.1.call-update) | async-done | bytes 1474576 | tf_op jit(solution)/shard_map/reduce_scatter | solution.py:48
  1015.9 0.0 copy-done
  1015.9 0.0 copy-done.3
  1015.9 0.0 copy-done.4
  1015.9 2.8 convolution_add_fusion
  1018.7 1.3 copy.11
  (2 shorter events, 0.0 us)
Async XLA Ops:
  6.5 1009.4 %copy-start = (bf16[3,3,256,256]{3,2,1,0:T(8,128)(2,1)S(1)}, bf16[3,3,256,256]{3,2,1,0:T(8,128)(2,1)}, u32[]{:S(2)}) copy-start(bf16[3,3,256,256]{3,2,1,0:T(8,128)(2,1)} %param.8) | copy-start | bytes 3538948
  6.5 1009.4 %reduce-scatter.2.cloned.1.call-start = ((), (), s32[]{:S(2)}) async-start(), calls=%async_computation.1 | async-start | bytes 190218240 | tf_op jit(solution)/shard_map/reduce_scatter | solution.py:48
  86.5 33.8 %copy-start.1 = (f32[8,8,128,256]{3,0,2,1:T(8,128)}, f32[8,8,128,256]{3,0,2,1:T(8,128)S(1)}, u32[]{:S(2)}) copy-start(f32[8,8,128,256]{3,0,2,1:T(8,128)S(1)} %concatenate.25) | copy-start | bytes 25165828
  93.3 27.0 %copy-start.2 = (f32[8,8,128,256]{3,0,2,1:T(8,128)}, f32[8,8,128,256]{3,0,2,1:T(8,128)S(1)}, u32[]{:S(2)}) copy-start(f32[8,8,128,256]{3,0,2,1:T(8,128)S(1)} %concatenate.28) | copy-start | bytes 25165828
  394.1 621.8 %copy-start.3 = (f32[256]{0:T(256)S(1)}, f32[256]{0:T(256)}, u32[]{:S(2)}) copy-start(f32[256]{0:T(256)} %param.7) | copy-start | bytes 3076
  394.1 621.8 %copy-start.4 = (f32[256]{0:T(256)S(1)}, f32[256]{0:T(256)}, u32[]{:S(2)}) copy-start(f32[256]{0:T(256)} %param.9) | copy-start | bytes 3076
Sparse Core Ops, SparseCore 0:
  394.3 621.5 reduce-scatter.1
where the time goes:
time: 1030 us
  waiting for transfers between devices  622 us (60%)
  local copies, waits for them, and re-layouts  181 us (18%)
  other arithmetic  155 us (15%)
  matrix products  55.7 us (5%)
  between operations  13.5 us (1%)
    reduce_scatter x1, waiting for transfers between devices, run_local(): lax.psum_scatter(windows, GROUP_AXES, scatter_dimension=0, tiled=False)  622 us
    transpose x1, other arithmetic, halo_tiles(): windows = windows.transpose(1, 3, 0, 2, 4, 5)  128 us
    transpose x1, local copies, waits for them, and re-layouts, halo_tiles(): windows = windows.transpose(1, 3, 0, 2, 4, 5)  122 us
    conv_general_dilated x1, matrix products, run_local(): lax.conv_general_dilated(x_in, w_conv1, (1, 1), 'SAME', dimension_numbers...  52.9 us
    squeeze x1, other arithmetic, halo_tiles(): left = jnp.concatenate([zero_col, grid[:, :, :, :-1, tile_w - 1]], axis=3)  27 us
    broadcast_in_dim x1, local copies, waits for them, and re-layouts, halo_tiles(): right[:, :, :, :, None]  23.9 us
  transfers between devices with their start and end apart: 1, of which 1 were waited for; matrix products, arithmetic and copies ran while one was open for 0% of the time, Pallas kernels for 0%

commit v1 on v0

v1 whole, which is shorter than its diff:
```python
import functools

import jax
import jax.numpy as jnp
from jax import lax
from jax.experimental import pallas as pl
from jax.experimental.pallas import tpu as pltpu
from jax.sharding import PartitionSpec as P

MESH = pl.DeviceIdType.MESH
GROUP_AXES = ("model", "cols")

N_DEV = 128
N_COLS = 16
HALVES = 2
W_ROWS = 10
PIX = 80
WIN = 12 * PIX
MID = 10 * PIX
C1 = 128
C2 = 256


def dot(a, b):
    return lax.dot_general(a, b, (((1,), (0,)), ((), ())), preferred_element_type=jnp.float32)


def dot_t(a, b):
    return lax.dot_general(a, b, (((0,), (0,)), ((), ())), preferred_element_type=jnp.float32)


def kernel(x_hbm, w1_ref, b1_ref, w2_hbm, b2_ref, out_ref,
           x_loc, pick, sel, place, s_w, s_x0, s_x1, r_w, r_w2, r_x0, r_x1,
           w1_mat, w2_mat, tmp, wtmp, xt, xs, mid, ys, inside, res,
           sem_x, sem_w2, send_w, send_x0, send_x1, send_d, recv_w, recv_x0, recv_x1, recv_d):
    m = lax.axis_index("model")
    c = lax.axis_index("cols")
    me = m * N_COLS + c
    core = m % 2

    def peer_of(step):
        dz = (2 + step // 32) % 4
        dy = (2 + (step // 8) % 4) % 4
        dx = (2 + (step // 2) % 4) % 4
        dk = 1 - step % 2
        px = (m // 2 + dx) % 4
        pk = (core + dk) % 2
        pz = (c // 4 + dz) % 4
        py = (c % 4 + dy) % 4
        return px * 2 + pk, pz * 4 + py

    SELF = 2 * 32 + 2 * 8 + 2 * 2 + 1

    def each_peer(body):
        def step(i, carry):
            body(*peer_of(i))
            return carry
        lax.fori_loop(0, SELF, step, 0)
        lax.fori_loop(SELF + 1, N_DEV, step, 0)

    barrier = pltpu.get_barrier_semaphore()

    def greet(pm, pc):
        pl.semaphore_signal(barrier, inc=1, device_id={"model": pm, "cols": pc}, device_id_type=MESH)

    each_peer(greet)
    get_x = pltpu.make_async_copy(x_hbm, x_loc, sem_x)
    get_x.start()
    get_w2 = pltpu.make_async_copy(w2_hbm, w2_mat, sem_w2)
    get_w2.start()

    for k in range(2):
        for j in range(4):
            tap = j + 5 * k
            for half in range(2):
                s_w[k, 2 * j + half : 2 * j + half + 1, :] = w1_ref[tap // 3, tap % 3 : tap % 3 + 1, half * 128 : half * 128 + 128]
        s_w[k, 8:9, :] = w1_ref[1, 1:2, k * 128 : k * 128 + 128]
        s_w[k, 9:10, :] = jnp.zeros((1, 128), jnp.bfloat16)

    for blk in range(4):
        lane = blk * 512 + lax.broadcasted_iota(jnp.int32, (1, 512), 1)
        img = lane % 4
        if blk < 2:
            row = (lane // 128) * 16 + (lane // 4) % 16
            at = img * 128 + row
        else:
            h = (lane // 4) % 4
            row = (lane // 128 - 8) * 16 + h - 2 + jnp.where(h >= 2, 16, 0)
            at = jnp.where((row >= 0) & (row < 128), img * 128 + row, -1)
        rows = lax.broadcasted_iota(jnp.int32, (512, 512), 0)
        pick[:, blk * 512 : blk * 512 + 512] = jnp.where(rows == at, 1.0, 0.0).astype(jnp.bfloat16)
    r_id = lax.broadcasted_iota(jnp.int32, (128, 256), 0)
    k_id = lax.broadcasted_iota(jnp.int32, (128, 256), 1)
    first = (r_id // 8) * 8 - 2
    s_id = r_id % 8
    main = (s_id < 6) & ((k_id == first + 2 * s_id) | (k_id == first + 2 * s_id + 1)) & (k_id < 128)
    edge0 = (s_id == 6) & (k_id >= 128 + jnp.maximum(first, 0)) & (k_id < 128 + first + 8)
    edge1 = (s_id == 7) & (k_id >= 128 + first + 8) & (k_id < 128 + first + 12)
    place[...] = jnp.where(main | edge0 | edge1, 1.0, 0.0).astype(jnp.bfloat16)
    p_id = lax.broadcasted_iota(jnp.int32, (MID, 128), 0)
    at_row = m * 16 - 1 + (p_id % PIX) // 4
    at_col = c * 8 - 1 + p_id // PIX
    inside[...] = jnp.where((at_row >= 0) & (at_row < 128) & (at_col >= 0) & (at_col < 128), 1.0, 0.0)

    get_x.wait()
    w_id = lax.broadcasted_iota(jnp.int32, (128, 512), 0)
    l_id = lax.broadcasted_iota(jnp.int32, (128, 512), 1) % 128
    keep_main = (l_id // 64) == (w_id % 2)
    keep_edge = (l_id // 16) == ((w_id + 2) % 8)
    for q, s_x in enumerate((s_x0, s_x1)):
        img = x_loc[4 * q : 4 * q + 4].reshape(512, 128)
        for blk in range(4):
            z = dot_t(img, pick[:, blk * 512 : blk * 512 + 512])
            keep = keep_main if blk < 2 else keep_edge
            top = 0 if blk < 2 else 128
            sel[top : top + 128, (blk % 2) * 512 : (blk % 2) * 512 + 512] = jnp.where(keep, z, 0.0).astype(jnp.bfloat16)
        for blk in range(2):
            t = dot(place[...], sel[:, blk * 512 : blk * 512 + 512]).astype(jnp.bfloat16)
            for r in range(4):
                tiles = t[:, r * 128 : r * 128 + 128].reshape(16, 8, 128)
                s_x[(blk * 4 + r) * 16 : (blk * 4 + r) * 16 + 16] = tiles

    pl.semaphore_wait(barrier, N_DEV - 1)

    def send(src, dst, send_sem, recv_sem, pm, pc):
        pltpu.make_async_remote_copy(src_ref=src, dst_ref=dst, send_sem=send_sem, recv_sem=recv_sem,
                                     device_id={"model": pm, "cols": pc}, device_id_type=MESH).start()

    each_peer(lambda pm, pc: send(s_w.at[pm % 2], r_w.at[me], send_w, recv_w, pm, pc))
    each_peer(lambda pm, pc: send(s_x0.at[pm * N_COLS + pc], r_x0.at[me], send_x0, recv_x0, pm, pc))
    each_peer(lambda pm, pc: send(s_x1.at[pm * N_COLS + pc], r_x1.at[me], send_x1, recv_x1, pm, pc))
    r_w[pl.ds(me, 1)] = s_w[pl.ds(core, 1)]
    r_x0[pl.ds(me, 1)] = s_x0[pl.ds(me, 1)]
    r_x1[pl.ds(me, 1)] = s_x1[pl.ds(me, 1)]

    def drain(ref, sem):
        part = ref.at[pl.ds(0, N_DEV - 1)]
        pltpu.make_async_copy(part, part, sem).wait()

    def unpack_w(ref, k):
        wtmp[...] = ref[...].astype(jnp.float32).reshape(N_DEV * W_ROWS, 128)
        for s in range(9):
            rows = wtmp[pl.ds(s, N_DEV, stride=W_ROWS), :].astype(jnp.bfloat16)
            if s == 8:
                w1_mat[pl.ds(4 * C1, C1), pl.ds(pl.multiple_of(k * 128, 128), 128)] = rows
            else:
                tap = 5 * k + s // 2
                w1_mat[pl.ds(pl.multiple_of(tap * C1, C1), C1), (s % 2) * 128 : (s % 2) * 128 + 128] = rows

    drain(r_w, recv_w)
    swap = pltpu.make_async_remote_copy(src_ref=r_w, dst_ref=r_w2, send_sem=send_d, recv_sem=recv_d,
                                        device_id={"model": m + 1 - 2 * core, "cols": c}, device_id_type=MESH)
    swap.start()
    unpack_w(r_w, core)
    swap.wait_recv()
    unpack_w(r_w2, 1 - core)
    get_w2.wait()

    for q, (r_x, recv_x) in enumerate(((r_x0, recv_x0), (r_x1, recv_x1))):
        drain(r_x, recv_x)
        tmp[...] = r_x[...].astype(jnp.float32).reshape(N_DEV * 8, 128)
        for s in range(8):
            t = tmp[pl.ds(s, N_DEV, stride=8), :].T
            if s < 6:
                for par in range(2):
                    at = (2 * s + par) * PIX + 8
                    xt[at : at + 64, :] = t[par * 64 : par * 64 + 64]
            else:
                for j in range(8 if s == 6 else 4):
                    at = ((s - 6) * 8 + j) * PIX
                    xt[at : at + 8, :] = t[16 * j : 16 * j + 8]
                    xt[at + 72 : at + 80, :] = t[16 * j + 8 : 16 * j + 16]
        for dh in range(3):
            n = WIN - (0 if dh == 0 else 16)
            xs[dh, 0:n, :] = xt[4 * dh : 4 * dh + n, :].astype(jnp.bfloat16)
            if dh:
                xs[dh, n:WIN, :] = jnp.zeros((16, C1), jnp.bfloat16)
                xs[dh, n : n + 8, :] = xt[n + 4 * dh : n + 4 * dh + 8, :].astype(jnp.bfloat16)
        half_m = MID // 2
        for mc in range(2):
            acc = None
            for pair in range(5):
                lhs = []
                for tap in range(2 * pair, min(2 * pair + 2, 9)):
                    dh, dw = tap // 3, tap % 3
                    lhs.append(xs[dh, dw * PIX + mc * half_m : dw * PIX + mc * half_m + half_m, :])
                lhs = jnp.concatenate(lhs, axis=1) if len(lhs) > 1 else lhs[0]
                part = dot(lhs, w1_mat[pair * 256 : pair * 256 + lhs.shape[1], :])
                acc = part if acc is None else acc + part
            act = jnp.maximum(acc + b1_ref[...], 0.0)
            ok = inside[mc * half_m : mc * half_m + half_m, :] > 0.0
            mid[mc * half_m : mc * half_m + half_m, 0:128] = jnp.where(ok, act[:, 0:128], 0.0)
            mid[mc * half_m : mc * half_m + half_m, 128:256] = jnp.where(ok, act[:, 128:256], 0.0)
        for dh in range(3):
            for wc in range(10):
                ys[dh, wc] = mid[wc * PIX + 4 * dh : wc * PIX + 4 * dh + 64, :].astype(jnp.bfloat16)
        acc = None
        for tap in range(9):
            dh, dw = tap // 3, tap % 3
            part = dot(ys[dh, dw : dw + 8].reshape(512, C2), w2_mat[dh, dw])
            acc = part if acc is None else acc + part
        full = acc + b2_ref[...]
        res[0] = full[:, 0:128]
        res[1] = full[:, 128:256]
        for h in range(16):
            for n in range(4):
                for half in range(2):
                    cols = slice(half * 128, half * 128 + 128)
                    out_ref[4 * q + n, h, :, cols] = res.at[half][pl.ds(h * 4 + n, 8, stride=64), :]

    def drain_send(ref, sem):
        part = ref.at[pl.ds(0, N_DEV - 1)]
        pltpu.make_async_copy(part, part, sem).wait()

    drain_send(r_w, send_w)
    drain_send(s_x0, send_x0)
    drain_send(s_x1, send_x1)
    swap.wait_send()


def solution(mesh):
    def run_local(x_in, w_conv1, b_conv1, w_conv2, b_conv2):
        bf, f32 = jnp.bfloat16, jnp.float32
        vmem = pl.BlockSpec(memory_space=pltpu.VMEM)
        hbm = pl.BlockSpec(memory_space=pl.ANY)
        dma = pltpu.SemaphoreType.DMA
        x = x_in.reshape(x_in.shape[:3])
        w1 = w_conv1.reshape(3, 3, 256)
        return pl.pallas_call(
            kernel,
            name="conv_pair",
            out_shape=jax.ShapeDtypeStruct((8, 16, 8, C2), f32),
            in_specs=[hbm, vmem, vmem, hbm, vmem],
            out_specs=vmem,
            scratch_shapes=[
                pltpu.VMEM((8, 128, 128), bf),
                pltpu.VMEM((512, 2048), bf),
                pltpu.VMEM((256, 1024), bf),
                pltpu.VMEM((128, 256), bf),
                pltpu.VMEM((2, W_ROWS, 128), bf),
                pltpu.VMEM((N_DEV, 8, 128), bf),
                pltpu.VMEM((N_DEV, 8, 128), bf),
                pltpu.VMEM((N_DEV, W_ROWS, 128), bf),
                pltpu.VMEM((N_DEV, W_ROWS, 128), bf),
                pltpu.VMEM((N_DEV, 8, 128), bf),
                pltpu.VMEM((N_DEV, 8, 128), bf),
                pltpu.VMEM((9 * C1, C2), bf),
                pltpu.VMEM((3, 3, C2, C2), bf),
                pltpu.VMEM((N_DEV * 8, 128), f32),
                pltpu.VMEM((N_DEV * W_ROWS, 128), f32),
                pltpu.VMEM((WIN, C1), f32),
                pltpu.VMEM((3, WIN, C1), bf),
                pltpu.VMEM((MID, C2), f32),
                pltpu.VMEM((3, 10, 64, C2), bf),
                pltpu.VMEM((MID, 128), f32),
                pltpu.VMEM((2, 512, 128), f32),
            ] + [dma] * 10,
            compiler_params=pltpu.CompilerParams(collective_id=0, has_side_effects=True, vmem_limit_bytes=60 << 20),
        )(x, w1, b_conv1.reshape(1, 256), w_conv2, b_conv2.reshape(1, 256))

    return jax.shard_map(
        run_local,
        mesh=mesh,
        in_specs=(P("data", None, None, GROUP_AXES), P(None, None, GROUP_AXES, None), P(), P(), P()),
        out_specs=P("data", "model", "cols", None),
        check_vma=False,
    )
```

time: 1030 us -> 44 us (0.04)
  waiting for transfers between devices: 622 us -> 0 us
  local copies, waits for them, and re-layouts: 181 us -> 2.27 us
  other arithmetic: 155 us -> 0 us
  matrix products: 55.7 us -> 0 us
  Pallas kernels: 0 us -> 41.6 us
  between operations: 13.5 us -> 0.01 us
    reduce_scatter x1 -> x0, waiting for transfers between devices: 622 us -> none  [run_local(): lax.psum_scatter(windows, GROUP_AXES, scatter_dimension=0, tiled=False)]
    transpose x1 -> x0, other arithmetic: 128 us -> none  [halo_tiles(): windows = windows.transpose(1, 3, 0, 2, 4, 5)]
    transpose x1 -> x0, local copies, waits for them, and re-layouts: 122 us -> none  [halo_tiles(): windows = windows.transpose(1, 3, 0, 2, 4, 5)]
    conv_general_dilated x2 -> x0, matrix products: 55.7 us -> none  [the longest x1 52.9 us: run_local(): lax.conv_general_dilated(x_in, w_conv1, (1, 1), 'SAME', dimension_numbers...]
    pallas_call x0 -> x1, Pallas kernels: none -> 41.6 us  [run_local(): pl.pallas_call(kernel, name='conv_pair', out_shape=jax.ShapeDtypeStruct((...]
    squeeze x1 -> x0, other arithmetic: 27 us -> none  [halo_tiles(): left = jnp.concatenate([zero_col, grid[:, :, :, :-1, tile_w - 1]], axis=3)]
    broadcast_in_dim x1 -> x0, local copies, waits for them, and re-layouts: 23.9 us -> none  [halo_tiles(): right[:, :, :, :, None]]
    squeeze x1 -> x0, local copies, waits for them, and re-layouts: 11.3 us -> none  [halo_tiles(): above = jnp.concatenate([zero_row, blocks[:, :-1, tile_h - 1]], axis=1)]
  transfers between devices with their start and end apart: 1 -> 0, of which waited for: 1 -> 0; matrix products, arithmetic and copies ran while one was open for 0% -> 0% of each run, Pallas kernels for 0% -> 0%
where the time goes in v1:
time: 44 us; the launch traced here: 43.8 us
  Pallas kernels  41.6 us (95%)
  local copies, waits for them, and re-layouts  2.27 us (5%)
    pallas_call x1, Pallas kernels, run_local(): pl.pallas_call(kernel, name='conv_pair', out_shape=jax.ShapeDtypeStruct((...  41.6 us
    unnamed x1, local copies, waits for them, and re-layouts  2.27 us

profile of v1, /device:TPU:1, one launch (start us, length us, event | category | flops | bytes accessed | tf_op | source)
XLA Modules:
  0.0 43.8 jit_solution(8348956288356602978)
XLA Ops:
  0.0 41.6 %conv_pair.1 = f32[8,16,8,256]{3,2,1,0:T(8,128)} custom-call(bf16[8,128,128]{2,1,0:T(8,128)(2,1)} %bitcast.4, bf16[3,3,256]{2,1,0:T(4,128)(2,1)} %bitcast.5, f32[1,256]{1,0:T(1,128)} %bitcast.6, bf16[3,3,256,256]{3,2,1,0:T(8,128)(2,1)} %w2_hbm.1, f32[1,256]{1,0:T(1,128)} %bitcast.7), custom_call_target="tpu_custom_call" | custom-call | tf_op jit(solution)/shard_map/conv_pair/pallas_call | solution.py:229
  41.6 2.3 %copy.7 = f32[8,16,8,256]{3,2,1,0:T(8,128)} copy(f32[8,16,8,256]{3,2,1,0:T(8,128)} %conv_pair.1) | data formatting | bytes 2097152

commit v2 on v1

v2 whole, which is shorter than its diff:
```python
import functools

import jax
import jax.numpy as jnp
from jax import lax
from jax.experimental import pallas as pl
from jax.experimental.pallas import tpu as pltpu
from jax.sharding import PartitionSpec as P

MESH = pl.DeviceIdType.MESH
GROUP_AXES = ("model", "cols")

N_DEV = 128
N_COLS = 16
HALVES = 2
PIX = 80
WIN = 12 * PIX
MID = 10 * PIX
C1 = 128
C2 = 256


def dot(a, b):
    return lax.dot_general(a, b, (((1,), (0,)), ((), ())), preferred_element_type=jnp.float32)


def dot_t(a, b):
    return lax.dot_general(a, b, (((0,), (0,)), ((), ())), preferred_element_type=jnp.float32)


def kernel(x_hbm, w1_hbm, b1_hbm, w2_hbm, b2_hbm, out_ref, ys, w2_mat,
           x_loc, w1_loc, b1_loc, b2_loc, pick, sel, place, s_w, s_t, s_x0, s_x1, r_w, r_w2, r_t, r_x0, r_x1,
           w1_mat, tmp, xt, xs, mid, inside, res,
           sem_x, sem_w1, sem_b, sem_w2, send_w, send_t, send_x0, send_x1, send_d,
           recv_w, recv_t, recv_x0, recv_x1, recv_d):
    m = lax.axis_index("model")
    c = lax.axis_index("cols")
    me = m * N_COLS + c
    core = m % 2

    get_x = pltpu.make_async_copy(x_hbm, x_loc, sem_x)
    get_x.start()
    get_w1 = pltpu.make_async_copy(w1_hbm, w1_loc, sem_w1)
    get_w1.start()
    get_b = (pltpu.make_async_copy(b1_hbm, b1_loc, sem_b.at[0]), pltpu.make_async_copy(b2_hbm, b2_loc, sem_b.at[1]))
    for get in get_b:
        get.start()
    get_w2 = pltpu.make_async_copy(w2_hbm, w2_mat, sem_w2)
    get_w2.start()

    pms = [((m // 2 + dx) % 4) * 2 + (core + dk) % 2 for dx in (2, 1, 3, 0) for dk in (1, 0)]

    def each_peer(body):
        def step(i, carry):
            tz, ty = i // 4, i % 4
            dz = (2 + tz) % 4 + (tz // 2) * (1 - 2 * (tz % 2))
            dy = (2 + ty) % 4 + (ty // 2) * (1 - 2 * (ty % 2))
            pc = ((c // 4 + dz) % 4) * 4 + (c % 4 + dy) % 4
            for pm in pms:
                body(pm, pc)
            return carry
        lax.fori_loop(0, 15, step, 0)
        for pm in pms[:-1]:
            body(pm, c)

    barrier = pltpu.get_barrier_semaphore()

    def greet(pm, pc):
        pl.semaphore_signal(barrier, inc=1, device_id={"model": pm, "cols": pc}, device_id_type=MESH)

    each_peer(greet)

    for blk in range(4):
        lane = blk * 512 + lax.broadcasted_iota(jnp.int32, (1, 512), 1)
        img = lane % 4
        if blk < 2:
            row = (lane // 128) * 16 + (lane // 4) % 16
            at = img * 128 + row
        else:
            h = (lane // 4) % 4
            row = (lane // 128 - 8) * 16 + h - 2 + jnp.where(h >= 2, 16, 0)
            at = jnp.where((row >= 0) & (row < 128), img * 128 + row, -1)
        rows = lax.broadcasted_iota(jnp.int32, (512, 512), 0)
        pick[:, blk * 512 : blk * 512 + 512] = jnp.where(rows == at, 1.0, 0.0).astype(jnp.bfloat16)
    r_id = lax.broadcasted_iota(jnp.int32, (128, 256), 0)
    k_id = lax.broadcasted_iota(jnp.int32, (128, 256), 1)
    first = (r_id // 8) * 8 - 2
    s_id = r_id % 8
    main = (s_id < 6) & ((k_id == first + 2 * s_id) | (k_id == first + 2 * s_id + 1)) & (k_id < 128)
    edge0 = (s_id == 6) & (k_id >= 128 + jnp.maximum(first, 0)) & (k_id < 128 + first + 8)
    edge1 = (s_id == 7) & (k_id >= 128 + first + 8) & (k_id < 128 + first + 12)
    place[...] = jnp.where(main | edge0 | edge1, 1.0, 0.0).astype(jnp.bfloat16)
    p_id = lax.broadcasted_iota(jnp.int32, (MID, 128), 0)
    at_row = m * 16 - 1 + (p_id % PIX) // 4
    at_col = c * 8 - 1 + p_id // PIX
    inside[...] = jnp.where((at_row >= 0) & (at_row < 128) & (at_col >= 0) & (at_col < 128), 1.0, 0.0)

    get_w1.wait()
    for tap in range(9):
        for half in range(2):
            row = w1_loc[tap // 3, tap % 3 : tap % 3 + 1, half * 128 : half * 128 + 128]
            if tap < 8:
                at = 2 * (tap % 4) + half
                s_w[tap // 4, at : at + 1, :] = row
            else:
                s_t[half : half + 1, :] = row

    pl.semaphore_wait(barrier, N_DEV - 1)

    def send(src, dst, send_sem, recv_sem, pm, pc):
        pltpu.make_async_remote_copy(src_ref=src, dst_ref=dst, send_sem=send_sem, recv_sem=recv_sem,
                                     device_id={"model": pm, "cols": pc}, device_id_type=MESH).start()

    def send_weights(pm, pc):
        send(s_w.at[pm % 2], r_w.at[me], send_w, recv_w, pm, pc)
        send(s_t, r_t.at[me], send_t, recv_t, pm, pc)

    each_peer(send_weights)

    get_x.wait()
    w_id = lax.broadcasted_iota(jnp.int32, (128, 512), 0)
    l_id = lax.broadcasted_iota(jnp.int32, (128, 512), 1) % 128
    keep_main = (l_id // 64) == (w_id % 2)
    keep_edge = (l_id // 16) == ((w_id + 2) % 8)
    for q, s_x in enumerate((s_x0, s_x1)):
        img = x_loc[4 * q : 4 * q + 4].reshape(512, 128)
        for blk in range(4):
            z = dot_t(img, pick[:, blk * 512 : blk * 512 + 512])
            keep = keep_main if blk < 2 else keep_edge
            top = 0 if blk < 2 else 128
            sel[top : top + 128, (blk % 2) * 512 : (blk % 2) * 512 + 512] = jnp.where(keep, z, 0.0).astype(jnp.bfloat16)
        for blk in range(2):
            t = dot(place[...], sel[:, blk * 512 : blk * 512 + 512]).astype(jnp.bfloat16)
            for r in range(4):
                tiles = t[:, r * 128 : r * 128 + 128].reshape(16, 8, 128)
                s_x[(blk * 4 + r) * 16 : (blk * 4 + r) * 16 + 16] = tiles

    each_peer(lambda pm, pc: send(s_x0.at[pm * N_COLS + pc], r_x0.at[me], send_x0, recv_x0, pm, pc))
    each_peer(lambda pm, pc: send(s_x1.at[pm * N_COLS + pc], r_x1.at[me], send_x1, recv_x1, pm, pc))
    r_w[pl.ds(me, 1)] = s_w[pl.ds(core, 1)]
    r_t[pl.ds(me, 1)] = s_t[...].reshape(1, 2, 128)
    r_x0[pl.ds(me, 1)] = s_x0[pl.ds(me, 1)]
    r_x1[pl.ds(me, 1)] = s_x1[pl.ds(me, 1)]

    def drain(ref, sem):
        part = ref.at[pl.ds(0, N_DEV - 1)]
        pltpu.make_async_copy(part, part, sem).wait()

    def unpack_w(ref, k):
        tmp[...] = ref[...].astype(jnp.float32).reshape(N_DEV * 8, 128)
        for s in range(8):
            rows = tmp[pl.ds(s, N_DEV, stride=8), :].astype(jnp.bfloat16)
            at = pl.multiple_of((4 * k + s // 2) * C1, C1)
            w1_mat[pl.ds(at, C1), (s % 2) * 128 : (s % 2) * 128 + 128] = rows

    drain(r_w, recv_w)
    swap = pltpu.make_async_remote_copy(src_ref=r_w, dst_ref=r_w2, send_sem=send_d, recv_sem=recv_d,
                                        device_id={"model": m + 1 - 2 * core, "cols": c}, device_id_type=MESH)
    swap.start()
    unpack_w(r_w, core)
    drain(r_t, recv_t)
    tmp[0 : 2 * N_DEV] = r_t[...].astype(jnp.float32).reshape(N_DEV * 2, 128)
    for half in range(2):
        w1_mat[8 * C1 : 9 * C1, half * 128 : half * 128 + 128] = tmp[pl.ds(half, N_DEV, stride=2), :].astype(jnp.bfloat16)
    swap.wait_recv()
    unpack_w(r_w2, 1 - core)
    for get in get_b:
        get.wait()
    get_w2.wait()

    for q, (r_x, recv_x) in enumerate(((r_x0, recv_x0), (r_x1, recv_x1))):
        drain(r_x, recv_x)
        tmp[...] = r_x[...].astype(jnp.float32).reshape(N_DEV * 8, 128)
        for s in range(8):
            t = tmp[pl.ds(s, N_DEV, stride=8), :].T
            if s < 6:
                for par in range(2):
                    at = (2 * s + par) * PIX + 8
                    xt[at : at + 64, :] = t[par * 64 : par * 64 + 64]
            else:
                for j in range(8 if s == 6 else 4):
                    at = ((s - 6) * 8 + j) * PIX
                    xt[at : at + 8, :] = t[16 * j : 16 * j + 8]
                    xt[at + 72 : at + 80, :] = t[16 * j + 8 : 16 * j + 16]
        for dh in range(3):
            n = WIN - (0 if dh == 0 else 16)
            xs[dh, 0:n, :] = xt[4 * dh : 4 * dh + n, :].astype(jnp.bfloat16)
            if dh:
                xs[dh, n:WIN, :] = jnp.zeros((16, C1), jnp.bfloat16)
                xs[dh, n : n + 8, :] = xt[n + 4 * dh : n + 4 * dh + 8, :].astype(jnp.bfloat16)
        half_m = MID // 2
        for mc in range(2):
            acc = None
            for pair in range(5):
                lhs = []
                for tap in range(2 * pair, min(2 * pair + 2, 9)):
                    dh, dw = tap // 3, tap % 3
                    lhs.append(xs[dh, dw * PIX + mc * half_m : dw * PIX + mc * half_m + half_m, :])
                lhs = jnp.concatenate(lhs, axis=1) if len(lhs) > 1 else lhs[0]
                part = dot(lhs, w1_mat[pair * 256 : pair * 256 + lhs.shape[1], :])
                acc = part if acc is None else acc + part
            act = jnp.maximum(acc + b1_loc[...], 0.0)
            ok = inside[mc * half_m : mc * half_m + half_m, :] > 0.0
            mid[mc * half_m : mc * half_m + half_m, 0:128] = jnp.where(ok, act[:, 0:128], 0.0)
            mid[mc * half_m : mc * half_m + half_m, 128:256] = jnp.where(ok, act[:, 128:256], 0.0)
        for dh in range(3):
            for wc in range(10):
                ys[dh, wc] = mid[wc * PIX + 4 * dh : wc * PIX + 4 * dh + 64, :].astype(jnp.bfloat16)
        if q == 0:
            conv_two(ys, w2_mat, b2_loc, res)
            unscramble(res, out_ref)

    def drain_send(ref, sem):
        part = ref.at[pl.ds(0, N_DEV - 1)]
        pltpu.make_async_copy(part, part, sem).wait()

    drain_send(r_w, send_w)
    drain_send(r_t, send_t)
    drain_send(s_x0, send_x0)
    drain_send(s_x1, send_x1)
    swap.wait_send()


def conv_two(ys, w2_mat, b2_ref, res):
    acc = None
    for tap in range(9):
        dh, dw = tap // 3, tap % 3
        part = dot(ys[dh, dw : dw + 8].reshape(512, C2), w2_mat[dh, dw])
        acc = part if acc is None else acc + part
    full = acc + b2_ref[...]
    res[0] = full[:, 0:128]
    res[1] = full[:, 128:256]


def unscramble(res, out_ref):
    for n in range(4):
        for h in range(16):
            for half in range(2):
                out_ref[n, h, :, half * 128 : half * 128 + 128] = res.at[half][pl.ds(h * 4 + n, 8, stride=64), :]


def kernel_two(out0, ys, w2_mat, b2_ref, out_hbm, out1, res, sem):
    put0 = pltpu.make_async_copy(out0, out_hbm.at[0:4], sem.at[0])
    put0.start()
    conv_two(ys, w2_mat, b2_ref, res)
    unscramble(res, out1)
    put1 = pltpu.make_async_copy(out1, out_hbm.at[4:8], sem.at[1])
    put1.start()
    put0.wait()
    put1.wait()


def solution(mesh):
    def run_local(x_in, w_conv1, b_conv1, w_conv2, b_conv2):
        bf, f32 = jnp.bfloat16, jnp.float32
        vmem = pl.BlockSpec(memory_space=pltpu.VMEM)
        hbm = pl.BlockSpec(memory_space=pltpu.HBM)
        dma = pltpu.SemaphoreType.DMA
        x = x_in.reshape(x_in.shape[:3])
        w1 = w_conv1.reshape(3, 3, 256)
        b2 = b_conv2.reshape(1, 256)
        out0, ys, w2 = pl.pallas_call(
            kernel,
            name="conv_pair",
            out_shape=[
                jax.ShapeDtypeStruct((4, 16, 8, C2), f32),
                jax.ShapeDtypeStruct((3, 10, 64, C2), bf),
                jax.ShapeDtypeStruct((3, 3, C2, C2), bf),
            ],
            in_specs=[hbm] * 5,
            out_specs=[vmem] * 3,
            scratch_shapes=[
                pltpu.VMEM((8, 128, 128), bf),
                pltpu.VMEM((3, 3, C2), bf),
                pltpu.VMEM((1, C2), f32),
                pltpu.VMEM((1, C2), f32),
                pltpu.VMEM((512, 2048), bf),
                pltpu.VMEM((256, 1024), bf),
                pltpu.VMEM((128, 256), bf),
                pltpu.VMEM((2, 8, 128), bf),
                pltpu.VMEM((2, 128), bf),
                pltpu.VMEM((N_DEV, 8, 128), bf),
                pltpu.VMEM((N_DEV, 8, 128), bf),
                pltpu.VMEM((N_DEV, 8, 128), bf),
                pltpu.VMEM((N_DEV, 8, 128), bf),
                pltpu.VMEM((N_DEV, 2, 128), bf),
                pltpu.VMEM((N_DEV, 8, 128), bf),
                pltpu.VMEM((N_DEV, 8, 128), bf),
                pltpu.VMEM((9 * C1, C2), bf),
                pltpu.VMEM((N_DEV * 8, 128), f32),
                pltpu.VMEM((WIN, C1), f32),
                pltpu.VMEM((3, WIN, C1), bf),
                pltpu.VMEM((MID, C2), f32),
                pltpu.VMEM((MID, 128), f32),
                pltpu.VMEM((2, 512, 128), f32),
                dma, dma, pltpu.SemaphoreType.DMA((2,)),
            ] + [dma] * 11,
            compiler_params=pltpu.CompilerParams(collective_id=0, has_side_effects=True, vmem_limit_bytes=24 << 20),
        )(*(pltpu.with_memory_space_constraint(a, pltpu.HBM) for a in (x, w1, b_conv1.reshape(1, 256), w_conv2, b2)))
        return pl.pallas_call(
            kernel_two,
            name="conv_last",
            out_shape=jax.ShapeDtypeStruct((8, 16, 8, C2), f32),
            in_specs=[vmem] * 4,
            out_specs=hbm,
            scratch_shapes=[pltpu.VMEM((4, 16, 8, C2), f32), pltpu.VMEM((2, 512, 128), f32), pltpu.SemaphoreType.DMA((2,))],
            compiler_params=pltpu.CompilerParams(vmem_limit_bytes=24 << 20),
        )(out0, ys, w2, b2)

    return jax.shard_map(
        run_local,
        mesh=mesh,
        in_specs=(P("data", None, None, GROUP_AXES), P(None, None, GROUP_AXES, None), P(), P(), P()),
        out_specs=P("data", "model", "cols", None),
        check_vma=False,
    )
```

time: 44 us -> 30.8 us (0.70)
  Pallas kernels: 41.6 us -> 30.7 us
  local copies, waits for them, and re-layouts: 2.27 us -> 0.01 us
    pallas_call x1 -> x2, Pallas kernels: 41.6 us -> 30.7 us  [the longest x1 28.7 us: run_local(): pl.pallas_call(kernel, name='conv_pair', out_shape=[jax.ShapeDtypeStruct(...]
    unnamed x1 -> x2, local copies, waits for them, and re-layouts: 2.27 us -> 0.01 us
where the time goes in v2:
time: 30.8 us; the launch traced here: 30.7 us
  Pallas kernels  30.7 us (100%)
    pallas_call x1, Pallas kernels, run_local(): pl.pallas_call(kernel, name='conv_pair', out_shape=[jax.ShapeDtypeStruct(...  28.7 us
    pallas_call x1, Pallas kernels, run_local(): pl.pallas_call(kernel_two, name='conv_last', out_shape=jax.ShapeDtypeStru...  1.97 us

profile of v2, /device:TPU:1, one launch (start us, length us, event | category | flops | bytes accessed | tf_op | source)
XLA Modules:
  0.0 30.7 jit_solution(16202765676608508535)
XLA Ops:
  0.0 0.0 copy-start
  0.0 28.7 %conv_pair.1 = (f32[4,16,8,256]{3,2,1,0:T(8,128)S(1)}, bf16[3,10,64,256]{3,2,1,0:T(8,128)(2,1)S(1)}, bf16[3,3,256,256]{3,2,1,0:T(8,128)(2,1)S(1)}) custom-call(bf16[8,128,128]{2,1,0:T(8,128)(2,1)} %bitcast.6, bf16[3,3,256]{2,1,0:T(4,128)(2,1)} %bitcast.7, f32[1,256]{1,0:T(1,128)} %bitcast.8, bf16[3,3,256,256]{3,2,1,0:T(8,128)(2,1)} %w2_hbm.1, f32[1,256]{1,0:T(1,128)} %bitcast.4), custom_call_target="tpu_custom_call" | custom-call | tf_op jit(solution)/shard_map/conv_pair/pallas_call | solution.py:262
  28.7 0.0 copy-done
  28.8 2.0 %conv_last.1 = f32[8,16,8,256]{3,2,1,0:T(8,128)} custom-call(f32[4,16,8,256]{3,2,1,0:T(8,128)S(1)} %get-tuple-element.8.out0, bf16[3,10,64,256]{3,2,1,0:T(8,128)(2,1)S(1)} %get-tuple-element.9.ys, bf16[3,3,256,256]{3,2,1,0:T(8,128)(2,1)S(1)} %get-tuple-element.10.w2_mat, f32[1,256]{1,0:T(1,128)S(1)} %bitcast.5), custom_call_target="tpu_custom_call" | custom-call | tf_op jit(solution)/shard_map/conv_last/pallas_call | solution.py:300
Async XLA Ops:
  0.0 28.8 %copy-start = (f32[256]{0:T(256)S(1)}, f32[256]{0:T(256)}, u32[]{:S(2)}) copy-start(f32[256]{0:T(256)} %param.9) | copy-start | bytes 3076

commit v3 on v0

v3 whole, which is shorter than its diff:
```python
import collections
import functools

import jax
import jax.numpy as jnp
from jax import lax
from jax.experimental import pallas as pl
from jax.experimental.pallas import tpu as pltpu
from jax.sharding import PartitionSpec as P

MESH = pl.DeviceIdType.MESH
GROUP_AXES = ("model", "cols")

N_DEV = 128
N_COLS = 16
COL = 160
MID_COL = 144
OUT_COL = 136
C1 = 128
C2 = 256
HOPS = (0, 1, 2, 1)


def peer_order():
    def links(shift):
        used = collections.Counter()
        for axis, d in enumerate(shift[:3]):
            if d in (1, 2):
                used[axis, 0] += 1
            if d in (3, 2):
                used[axis, 1] += 1
        return used

    shifts = [(dx, dy, dz, dk) for dx in range(4) for dy in range(4) for dz in range(4) for dk in range(2)][1:]
    load, order = collections.Counter(), []
    for tail in range(4, -1, -1):
        rest = [s for s in shifts if HOPS[s[1]] + HOPS[s[2]] == tail]
        while rest:
            def cost(s):
                new = load + links(s)
                return max(new.values(), default=0) * 100 + sum(v * v for v in new.values()) * 0.01
            best = min(rest, key=cost)
            rest.remove(best)
            order.append(best)
            load += links(best)
    return order


ORDER = peer_order()


def dot(a, b):
    return lax.dot_general(a, b, (((1,), (0,)), ((), ())), preferred_element_type=jnp.float32)


def kernel(x_hbm, w1_hbm, b1_hbm, w2_hbm, b2_hbm, out_ref,
           x_loc, w1_loc, b1_loc, b2_loc, w2_mat, turned, pick, sel, place, s_w, s_x, r_w, r_w2, r_x,
           w1_mat, tmp, edge, xs0, xs8, ys0, ys8, inside, res,
           sem_x, sem_w1, sem_b, sem_w2, send_w, send_x, send_d, recv_w, recv_x, recv_d):
    m = lax.axis_index("model")
    c = lax.axis_index("cols")
    me = m * N_COLS + c
    core = m % 2

    get_x = pltpu.make_async_copy(x_hbm, x_loc, sem_x)
    get_x.start()
    get_w1 = pltpu.make_async_copy(w1_hbm, w1_loc, sem_w1)
    get_w1.start()
    get_b = (pltpu.make_async_copy(b1_hbm, b1_loc, sem_b.at[0]), pltpu.make_async_copy(b2_hbm, b2_loc, sem_b.at[1]))
    for get in get_b:
        get.start()
    get_w2 = pltpu.make_async_copy(w2_hbm, w2_mat, sem_w2)
    get_w2.start()

    cores = (core, 1 - core)
    models = [[((m // 2 + dx) % 4) * 2 + k for k in cores] for dx in range(4)]
    cols_y = [(c % 4 + dy) % 4 for dy in range(4)]
    cols = [[((c // 4 + dz) % 4) * 4 + y for y in cols_y] for dz in range(4)]

    def each_peer(body):
        for dx, dy, dz, dk in ORDER:
            body(models[dx][dk], cols[dz][dy], cores[dk])

    barrier = pltpu.get_barrier_semaphore()

    def greet(pm, pc, pk):
        pl.semaphore_signal(barrier, inc=1, device_id={"model": pm, "cols": pc}, device_id_type=MESH)

    each_peer(greet)

    for blk in range(4):
        lane = blk * 512 + lax.broadcasted_iota(jnp.int32, (1, 512), 1)
        img = lane % 8
        if blk < 2:
            row = (lane // 128) * 16 + (lane // 8) % 16
        else:
            h = (lane // 8) % 4
            row = (lane // 128 - 8) * 16 + h - 2 + jnp.where(h >= 2, 16, 0)
        at = jnp.where((row >= 0) & (row < 128), img * 128 + row, -1)
        for pair in range(4):
            rows = pair * 256 + lax.broadcasted_iota(jnp.int32, (256, 512), 0)
            pick[pair * 256 : pair * 256 + 256, blk * 512 : blk * 512 + 512] = jnp.where(rows == at, 1.0, 0.0).astype(jnp.bfloat16)
    r_id = lax.broadcasted_iota(jnp.int32, (256, 256), 0)
    k_id = lax.broadcasted_iota(jnp.int32, (256, 256), 1)
    first = (r_id // 16) * 8 - 2
    s_id = r_id % 16
    main = (s_id < 12) & (k_id == first + s_id) & (k_id < 128)
    from_col = first + 4 * (s_id - 12)
    border = (s_id >= 12) & (s_id < 15) & (k_id >= 128 + jnp.maximum(from_col, 0)) & (k_id < 132 + from_col)
    place[...] = jnp.where(main | border, 1.0, 0.0).astype(jnp.bfloat16)
    p_id = lax.broadcasted_iota(jnp.int32, (10 * MID_COL, 128), 0)
    at_row = m * 16 - 1 + (p_id % MID_COL) // 8
    at_col = c * 8 - 1 + p_id // MID_COL
    inside[...] = jnp.where((at_row >= 0) & (at_row < 128) & (at_col >= 0) & (at_col < 128), 1.0, 0.0).reshape(10, MID_COL, 128)

    get_w1.wait()
    for k in range(2):
        for j in range(4):
            tap = 4 * k + j
            s_w[k, j] = jnp.concatenate([w1_loc[tap // 3, tap % 3 : tap % 3 + 1, half * 128 : half * 128 + 128] for half in range(2)])
        last = w1_loc[2, 2:3, k * 128 : k * 128 + 128]
        s_w[k, 4] = jnp.concatenate([last, jnp.zeros_like(last)])

    get_x.wait()
    for n in range(8):
        turned[:, n * 128 : n * 128 + 128] = x_loc[n].T
    w_id = lax.broadcasted_iota(jnp.int32, (128, 256), 0)
    l_id = lax.broadcasted_iota(jnp.int32, (128, 256), 1) % 128
    keep = (l_id // 32) == ((w_id + 2) % 4)
    for blk in range(8):
        z = None
        for pair in range(4):
            term = dot(turned[:, pair * 256 : pair * 256 + 256], pick[pair * 256 : pair * 256 + 256, blk * 256 : blk * 256 + 256])
            z = term if z is None else z + term
        if blk >= 4:
            z = jnp.where(keep, z, 0.0)
        top = 0 if blk < 4 else 128
        sel[top : top + 128, (blk % 4) * 256 : (blk % 4) * 256 + 256] = z.astype(jnp.bfloat16)
    for blk in range(4):
        t = dot(place[...], sel[:, blk * 256 : blk * 256 + 256])
        for r in range(2):
            tiles = t[:, r * 128 : r * 128 + 128].reshape(16, 2, 8, 128).astype(jnp.bfloat16)
            s_x[(blk * 2 + r) * 16 : (blk * 2 + r) * 16 + 16] = tiles

    pl.semaphore_wait(barrier, N_DEV - 1)

    def send(src, dst, send_sem, recv_sem, pm, pc):
        pltpu.make_async_remote_copy(src_ref=src, dst_ref=dst, send_sem=send_sem, recv_sem=recv_sem,
                                     device_id={"model": pm, "cols": pc}, device_id_type=MESH).start()

    each_peer(lambda pm, pc, pk: send(s_w.at[pk], r_w.at[me], send_w, recv_w, pm, pc))
    each_peer(lambda pm, pc, pk: send(s_x.at[pm * N_COLS + pc], r_x.at[me], send_x, recv_x, pm, pc))
    r_w[pl.ds(me, 1)] = s_w[pl.ds(core, 1)]
    r_x[pl.ds(me, 1)] = s_x[pl.ds(me, 1)]

    def drain(ref, sem):
        part = ref.at[pl.ds(0, N_DEV - 1)]
        pltpu.make_async_copy(part, part, sem).wait()

    def unpack_w(ref, k):
        for j in range(5):
            tmp[0, 0 : 2 * N_DEV] = ref[:, j].astype(jnp.float32).reshape(N_DEV * 2, 128)
            for half in range(2 if j < 4 else 1):
                rows = tmp.at[0][pl.ds(half, N_DEV, stride=2), :].astype(jnp.bfloat16)
                if j < 4:
                    at = pl.multiple_of((4 * k + j) * C1, C1)
                    w1_mat[pl.ds(at, C1), half * 128 : half * 128 + 128] = rows
                else:
                    w1_mat[8 * C1 : 9 * C1, pl.ds(pl.multiple_of(k * 128, 128), 128)] = rows

    drain(r_w, recv_w)
    swap = pltpu.make_async_remote_copy(src_ref=r_w, dst_ref=r_w2, send_sem=send_d, recv_sem=recv_d,
                                        device_id={"model": m + 1 - 2 * core, "cols": c}, device_id_type=MESH)
    swap.start()
    unpack_w(r_w, core)
    swap.wait_recv()
    unpack_w(r_w2, 1 - core)
    for get in get_b:
        get.wait()
    get_w2.wait()

    drain(r_x, recv_x)
    for half in range(2):
        tmp[half] = r_x[:, half].astype(jnp.float32).reshape(N_DEV * 8, 128)

    def pixels(s):
        return tmp.at[s // 8][pl.ds(s % 8, N_DEV, stride=8), :].T

    for s in range(12, 15):
        edge[s - 12] = pixels(s)
    for w in range(12):
        top = (w % 4) * 32
        col = jnp.concatenate([edge[w // 4, top : top + 16], pixels(w), edge[w // 4, top + 16 : top + 32]])
        xs0[w] = col.astype(jnp.bfloat16)
        xs8[w] = col[8 : 8 + MID_COL].astype(jnp.bfloat16)

    for lo, hi in ((0, 3), (3, 5), (5, 8), (8, 10)):
        acc = None
        for pair in range(5):
            lhs = []
            for tap in range(2 * pair, min(2 * pair + 2, 9)):
                dh, dw = tap // 3, tap % 3
                src = xs8 if dh == 1 else xs0
                top = 16 if dh == 2 else 0
                lhs.append(src[lo + dw : hi + dw, top : top + MID_COL].reshape((hi - lo) * MID_COL, C1))
            lhs = jnp.concatenate(lhs, axis=1) if len(lhs) > 1 else lhs[0]
            term = dot(lhs, w1_mat[pair * 256 : pair * 256 + lhs.shape[1], :])
            acc = term if acc is None else acc + term
        act = jnp.maximum(acc + b1_loc[...], 0.0).reshape(hi - lo, MID_COL, C2)
        for half in range(2):
            part = slice(half * 128, half * 128 + 128)
            real = jnp.where(inside[lo:hi] > 0.0, act[:, :, part], 0.0)
            ys0[lo:hi, :, part] = real.astype(jnp.bfloat16)
            ys8[lo:hi, :, part] = real[:, 8:136].astype(jnp.bfloat16)

    for lo in range(0, 8, 2):
        acc = None
        for tap in range(9):
            dh, dw = tap // 3, tap % 3
            src = ys8 if dh == 1 else ys0
            top = 16 if dh == 2 else 0
            term = dot(src[lo + dw : lo + dw + 2, top : top + 128].reshape(256, C2), w2_mat[dh, dw])
            acc = term if acc is None else acc + term
        full = acc + b2_loc[...]
        for w in range(2):
            for half in range(2):
                res[half, (lo + w) * OUT_COL : (lo + w) * OUT_COL + 128] = full[w * 128 : w * 128 + 128, half * 128 : half * 128 + 128]
    for n in range(8):
        for h in range(16):
            for half in range(2):
                out_ref[n, h, :, half * 128 : half * 128 + 128] = res.at[half][pl.ds(h * 8 + n, 8, stride=OUT_COL), :]

    drain(r_w, send_w)
    drain(s_x, send_x)
    swap.wait_send()


def put_out(out_vmem, out_hbm, sem):
    put = pltpu.make_async_copy(out_vmem, out_hbm, sem)
    put.start()
    put.wait()


def solution(mesh):
    def run_local(x_in, w_conv1, b_conv1, w_conv2, b_conv2):
        bf, f32 = jnp.bfloat16, jnp.float32
        vmem = pl.BlockSpec(memory_space=pltpu.VMEM)
        hbm = pl.BlockSpec(memory_space=pltpu.HBM)
        dma = pltpu.SemaphoreType.DMA
        operands = (x_in.reshape(x_in.shape[:3]), w_conv1.reshape(3, 3, C2), b_conv1.reshape(1, C2), w_conv2, b_conv2.reshape(1, C2))
        out = pl.pallas_call(
            kernel,
            name="conv_pair",
            out_shape=jax.ShapeDtypeStruct((8, 16, 8, C2), f32),
            in_specs=[hbm] * 5,
            out_specs=vmem,
            scratch_shapes=[
                pltpu.VMEM((8, 128, 128), bf),
                pltpu.VMEM((3, 3, C2), bf),
                pltpu.VMEM((1, C2), f32),
                pltpu.VMEM((1, C2), f32),
                pltpu.VMEM((3, 3, C2, C2), bf),
                pltpu.VMEM((128, 1024), bf),
                pltpu.VMEM((1024, 2048), bf),
                pltpu.VMEM((256, 1024), bf),
                pltpu.VMEM((256, 256), bf),
                pltpu.VMEM((2, 5, 2, 128), bf),
                pltpu.VMEM((N_DEV, 2, 8, 128), bf),
                pltpu.VMEM((N_DEV, 5, 2, 128), bf),
                pltpu.VMEM((N_DEV, 5, 2, 128), bf),
                pltpu.VMEM((N_DEV, 2, 8, 128), bf),
                pltpu.VMEM((9 * C1, C2), bf),
                pltpu.VMEM((2, N_DEV * 8, 128), f32),
                pltpu.VMEM((3, 128, 128), f32),
                pltpu.VMEM((12, COL, C1), bf),
                pltpu.VMEM((12, MID_COL, C1), bf),
                pltpu.VMEM((10, MID_COL, C2), bf),
                pltpu.VMEM((10, 128, C2), bf),
                pltpu.VMEM((10, MID_COL, 128), f32),
                pltpu.VMEM((2, 8 * OUT_COL, 128), f32),
                dma, dma, pltpu.SemaphoreType.DMA((2,)), dma,
                dma, dma, dma, dma, dma, dma,
            ],
            compiler_params=pltpu.CompilerParams(collective_id=0, has_side_effects=True, vmem_limit_bytes=24 << 20),
        )(*(pltpu.with_memory_space_constraint(a, pltpu.HBM) for a in operands))
        return pl.pallas_call(
            put_out,
            name="put_out",
            out_shape=jax.ShapeDtypeStruct((8, 16, 8, C2), f32),
            in_specs=[vmem],
            out_specs=hbm,
            scratch_shapes=[dma],
            compiler_params=pltpu.CompilerParams(vmem_limit_bytes=24 << 20),
        )(out)

    return jax.shard_map(
        run_local,
        mesh=mesh,
        in_specs=(P("data", None, None, GROUP_AXES), P(None, None, GROUP_AXES, None), P(), P(), P()),
        out_specs=P("data", "model", "cols", None),
        check_vma=False,
    )
```

time: 1030 us -> 26.3 us (0.03)
  waiting for transfers between devices: 622 us -> 0 us
  local copies, waits for them, and re-layouts: 181 us -> 0 us
  other arithmetic: 155 us -> 0 us
  matrix products: 55.7 us -> 0 us
  Pallas kernels: 0 us -> 26.2 us
  between operations: 13.5 us -> 0.01 us
    reduce_scatter x1 -> x0, waiting for transfers between devices: 622 us -> none  [run_local(): lax.psum_scatter(windows, GROUP_AXES, scatter_dimension=0, tiled=False)]
    transpose x1 -> x0, other arithmetic: 128 us -> none  [halo_tiles(): windows = windows.transpose(1, 3, 0, 2, 4, 5)]
    transpose x1 -> x0, local copies, waits for them, and re-layouts: 122 us -> none  [halo_tiles(): windows = windows.transpose(1, 3, 0, 2, 4, 5)]
    conv_general_dilated x2 -> x0, matrix products: 55.7 us -> none  [the longest x1 52.9 us: run_local(): lax.conv_general_dilated(x_in, w_conv1, (1, 1), 'SAME', dimension_numbers...]
    squeeze x1 -> x0, other arithmetic: 27 us -> none  [halo_tiles(): left = jnp.concatenate([zero_col, grid[:, :, :, :-1, tile_w - 1]], axis=3)]
    pallas_call x0 -> x2, Pallas kernels: none -> 26.2 us  [the longest x1 25.2 us: run_local(): pl.pallas_call(kernel, name='conv_pair', out_shape=jax.ShapeDtypeStruct((...]
    broadcast_in_dim x1 -> x0, local copies, waits for them, and re-layouts: 23.9 us -> none  [halo_tiles(): right[:, :, :, :, None]]
    unnamed x11 -> x0, local copies, waits for them, and re-layouts: 12 us -> none
  transfers between devices with their start and end apart: 1 -> 0, of which waited for: 1 -> 0; matrix products, arithmetic and copies ran while one was open for 0% -> 0% of each run, Pallas kernels for 0% -> 0%
where the time goes in v3:
time: 26.3 us; the launch traced here: 26.2 us
  Pallas kernels  26.2 us (100%)
    pallas_call x1, Pallas kernels, run_local(): pl.pallas_call(kernel, name='conv_pair', out_shape=jax.ShapeDtypeStruct((...  25.2 us
    pallas_call x1, Pallas kernels, run_local(): pl.pallas_call(put_out, name='put_out', out_shape=jax.ShapeDtypeStruct((8...  0.98 us

profile of v3, /device:TPU:1, one launch (start us, length us, event | category | flops | bytes accessed | tf_op | source)
XLA Modules:
  0.0 26.2 jit_solution(3719904329145069705)
XLA Ops:
  0.0 25.2 %conv_pair.1.out_vmem = f32[8,16,8,256]{3,2,1,0:T(8,128)S(1)} custom-call(bf16[8,128,128]{2,1,0:T(8,128)(2,1)} %bitcast.4, bf16[3,3,256]{2,1,0:T(4,128)(2,1)} %bitcast.5, f32[1,256]{1,0:T(1,128)} %bitcast.6, bf16[3,3,256,256]{3,2,1,0:T(8,128)(2,1)} %w2_hbm.1, f32[1,256]{1,0:T(1,128)} %bitcast.7), custom_call_target="tpu_custom_call" | custom-call | tf_op jit(solution)/shard_map/conv_pair/pallas_call | solution.py:251
  25.2 1.0 %put_out.1 = f32[8,16,8,256]{3,2,1,0:T(8,128)} custom-call(f32[8,16,8,256]{3,2,1,0:T(8,128)S(1)} %conv_pair.1.out_vmem), custom_call_target="tpu_custom_call" | custom-call | tf_op jit(solution)/shard_map/put_out/pallas_call | solution.py:286

commit v4 on v3

v4 whole, which is shorter than its diff:
```python
import collections
import functools

import jax
import jax.numpy as jnp
from jax import lax
from jax.experimental import pallas as pl
from jax.experimental.pallas import tpu as pltpu
from jax.sharding import PartitionSpec as P

MESH = pl.DeviceIdType.MESH
GROUP_AXES = ("model", "cols")

N_DEV = 128
N_COLS = 16
COL = 160
MID_COL = 144
OUT_COL = 40
C1 = 128
C2 = 256
HOPS = (0, 1, 2, 1)


def greet_order():
    shifts = [(dx, dy, dz) for dx in range(4) for dy in range(4) for dz in range(4)][1:]
    return sorted(shifts, key=lambda s: (-HOPS[s[1]] - HOPS[s[2]], -HOPS[s[0]]))


def send_order():
    def key(msg):
        window, dx, dy, z, dk = msg
        return (z // 2, 11 * (z == 1) + 100 * window - 10 * HOPS[dy] + 0.1 * (3, 1, 0, 2)[dx] + 0.01 * dk)

    return sorted(((w, dx, dy, z, dk) for w in range(2) for dx in range(4) for dy in range(4) for z in range(4) for dk in range(2)), key=key)


GREET_ORDER = greet_order()
SEND_ORDER = send_order()
EARLY = ((0,), (2, 3))


def dot(a, b):
    return lax.dot_general(a, b, (((1,), (0,)), ((), ())), preferred_element_type=jnp.float32)


def kernel(x_hbm, w1_hbm, b1_hbm, w2_hbm, b2_hbm, out_ref, ys0, ys8, w2_mat,
           x_loc, w1_loc, b1_loc, b2_loc, turned, pick, sel, place, s_w, s_x, r_w, r_w2, r_x,
           w1_mat, tmp, edge, xs0, xs8, inside, res,
           heard, sem_x, sem_w1, sem_b, sem_w2, send_w, send_x, send_d, recv_w, recv_x, recv_d):
    m = lax.axis_index("model")
    c = lax.axis_index("cols")
    me = m * N_COLS + c
    core = m % 2

    get_x = pltpu.make_async_copy(x_hbm, x_loc, sem_x)
    get_x.start()
    get_w1 = pltpu.make_async_copy(w1_hbm, w1_loc, sem_w1)
    get_w1.start()
    get_b = (pltpu.make_async_copy(b1_hbm, b1_loc, sem_b.at[0]), pltpu.make_async_copy(b2_hbm, b2_loc, sem_b.at[1]))
    for get in get_b:
        get.start()
    get_w2 = pltpu.make_async_copy(w2_hbm, w2_mat, sem_w2)
    get_w2.start()

    cores = (core, 1 - core)
    models = [[((m // 2 + dx) % 4) * 2 + k for k in cores] for dx in range(4)]
    ys = [(c % 4 + dy) % 4 for dy in range(4)]
    my_z = c // 4
    zs = [((my_z + dz) % 4) * 4 for dz in range(4)]

    barrier = pltpu.get_barrier_semaphore()
    part = my_z // 2
    partner = {"model": m + 1 - 2 * core, "cols": c}
    for dx, dy, dz in GREET_ORDER:
        to = {"model": ((m // 2 + dx) % 4) * 2 + part, "cols": zs[dz] + ys[dy]}
        pl.semaphore_signal(barrier, inc=1, device_id=to, device_id_type=MESH)
    pl.semaphore_signal(barrier, inc=1, device_id=partner, device_id_type=MESH)

    def hear(which):
        @pl.when(core == which)
        def _():
            pl.semaphore_wait(barrier, 63 + 2 * ((core + part) % 2))
            pl.semaphore_signal(heard, inc=1, device_id=partner, device_id_type=MESH)

        @pl.when(core != which)
        def _():
            pl.semaphore_wait(heard, 1)

    for blk in range(4):
        lane = blk * 512 + lax.broadcasted_iota(jnp.int32, (1, 512), 1)
        img = lane % 8
        if blk < 2:
            row = (lane // 128) * 16 + (lane // 8) % 16
        else:
            h = (lane // 8) % 4
            row = (lane // 128 - 8) * 16 + h - 2 + jnp.where(h >= 2, 16, 0)
        at = jnp.where((row >= 0) & (row < 128), img * 128 + row, -1)
        for pair in range(4):
            rows = pair * 256 + lax.broadcasted_iota(jnp.int32, (256, 512), 0)
            pick[pair * 256 : pair * 256 + 256, blk * 512 : blk * 512 + 512] = jnp.where(rows == at, 1.0, 0.0).astype(jnp.bfloat16)
    r_id = lax.broadcasted_iota(jnp.int32, (256, 256), 0)
    k_id = lax.broadcasted_iota(jnp.int32, (256, 256), 1)
    first = (r_id // 16) * 8 - 2
    s_id = r_id % 16
    main = (s_id < 12) & (k_id == first + s_id) & (k_id < 128)
    from_col = first + 4 * (s_id - 12)
    border = (s_id >= 12) & (s_id < 15) & (k_id >= 128 + jnp.maximum(from_col, 0)) & (k_id < 132 + from_col)
    place[...] = jnp.where(main | border, 1.0, 0.0).astype(jnp.bfloat16)
    get_w1.wait()
    for k in range(2):
        for j in range(4):
            tap = 4 * k + j
            s_w[k, j] = jnp.concatenate([w1_loc[tap // 3, tap % 3 : tap % 3 + 1, half * 128 : half * 128 + 128] for half in range(2)])
        last = w1_loc[2, 2:3, k * 128 : k * 128 + 128]
        s_w[k, 4] = jnp.concatenate([last, jnp.zeros_like(last)])

    get_x.wait()
    for n in range(8):
        turned[:, n * 128 : n * 128 + 128] = x_loc[n].T
    w_id = lax.broadcasted_iota(jnp.int32, (128, 256), 0)
    l_id = lax.broadcasted_iota(jnp.int32, (128, 256), 1) % 128
    keep = (l_id // 32) == ((w_id + 2) % 4)
    for blk in range(8):
        z = None
        for pair in range(4):
            term = dot(turned[:, pair * 256 : pair * 256 + 256], pick[pair * 256 : pair * 256 + 256, blk * 256 : blk * 256 + 256])
            z = term if z is None else z + term
        if blk >= 4:
            z = jnp.where(keep, z, 0.0)
        top = 0 if blk < 4 else 128
        sel[top : top + 128, (blk % 4) * 256 : (blk % 4) * 256 + 256] = z.astype(jnp.bfloat16)
    for blk in range(4):
        t = dot(place[...], sel[:, blk * 256 : blk * 256 + 256])
        for r in range(2):
            tiles = t[:, r * 128 : r * 128 + 128].reshape(16, 2, 8, 128).astype(jnp.bfloat16)
            s_x[(blk * 2 + r) * 16 : (blk * 2 + r) * 16 + 16] = tiles


    def send(src, dst, send_sem, recv_sem, pm, pc):
        pltpu.make_async_remote_copy(src_ref=src, dst_ref=dst, send_sem=send_sem, recv_sem=recv_sem,
                                     device_id={"model": pm, "cols": pc}, device_id_type=MESH).start()

    for step, (window, dx, dy, z, dk) in enumerate(SEND_ORDER):
        if step % N_DEV == 0:
            hear(step // N_DEV)
        if window and SEND_ORDER[step - 1][0] == 0:
            for first_z in EARLY[step // N_DEV]:
                for k in (1, 0):
                    def send_early(pm=k, pc=first_z * 4):
                        send(s_x.at[pm * N_COLS + pc], r_x.at[me], send_x, recv_x, pm, pc)
                    pl.when(me != k * N_COLS + first_z * 4)(send_early)
        pm, pc = models[dx][dk], z * 4 + ys[dy]

        def send_one(window=window, pm=pm, pc=pc, pk=cores[dk]):
            if window:
                send(s_x.at[pm * N_COLS + pc], r_x.at[me], send_x, recv_x, pm, pc)
            else:
                send(s_w.at[pk], r_w.at[me], send_w, recv_w, pm, pc)

        if window and z in EARLY[z // 2]:
            sent = models[dx][0] // 2 + ys[dy] == 0
            skip = sent | (my_z == z) if dx == dy == dk == 0 else sent
            pl.when(jnp.logical_not(skip))(send_one)
        elif dx == dy == dk == 0:
            pl.when(my_z != z)(send_one)
        else:
            send_one()
    r_w[pl.ds(me, 1)] = s_w[pl.ds(core, 1)]
    r_x[pl.ds(me, 1)] = s_x[pl.ds(me, 1)]

    at_row = m * 16 - 1 + lax.broadcasted_iota(jnp.int32, (10, MID_COL, 128), 1) // 8
    at_col = c * 8 - 1 + lax.broadcasted_iota(jnp.int32, (10, MID_COL, 128), 0)
    inside[...] = jnp.where((at_row >= 0) & (at_row < 128) & (at_col >= 0) & (at_col < 128), 1.0, 0.0)

    def drain(ref, sem):
        part = ref.at[pl.ds(0, N_DEV - 1)]
        pltpu.make_async_copy(part, part, sem).wait()

    def unpack_w(ref, k):
        for j in range(5):
            tmp[0, 0 : 2 * N_DEV] = ref[:, j].astype(jnp.float32).reshape(N_DEV * 2, 128)
            for half in range(2 if j < 4 else 1):
                rows = tmp.at[0][pl.ds(half, N_DEV, stride=2), :].astype(jnp.bfloat16)
                if j < 4:
                    at = pl.multiple_of((4 * k + j) * C1, C1)
                    w1_mat[pl.ds(at, C1), half * 128 : half * 128 + 128] = rows
                else:
                    w1_mat[8 * C1 : 9 * C1, pl.ds(pl.multiple_of(k * 128, 128), 128)] = rows

    drain(r_w, recv_w)
    swap = pltpu.make_async_remote_copy(src_ref=r_w, dst_ref=r_w2, send_sem=send_d, recv_sem=recv_d,
                                        device_id=partner, device_id_type=MESH)
    swap.start()
    unpack_w(r_w, core)
    swap.wait_recv()
    unpack_w(r_w2, 1 - core)
    for get in get_b:
        get.wait()
    get_w2.wait()

    drain(r_x, recv_x)
    for half in range(2):
        tmp[half] = r_x[:, half].astype(jnp.float32).reshape(N_DEV * 8, 128)

    def pixels(s):
        return tmp.at[s // 8][pl.ds(s % 8, N_DEV, stride=8), :].T

    for s in range(12, 15):
        edge[s - 12] = pixels(s)
    for w in range(12):
        top = (w % 4) * 32
        col = jnp.concatenate([edge[w // 4, top : top + 16], pixels(w), edge[w // 4, top + 16 : top + 32]])
        xs0[w] = col.astype(jnp.bfloat16)
        xs8[w] = col[8 : 8 + MID_COL].astype(jnp.bfloat16)

    before = None
    for top, rows in ((0, 48), (48, 32), (80, 32), (112, 32)):
        acc = None
        for pair in range(5):
            lhs = []
            for tap in range(2 * pair, min(2 * pair + 2, 9)):
                dh, dw = tap // 3, tap % 3
                src = xs8 if dh == 1 else xs0
                at = top + (16 if dh == 2 else 0)
                lhs.append(src[dw : dw + 10, at : at + rows].reshape(10 * rows, C1))
            lhs = jnp.concatenate(lhs, axis=1) if len(lhs) > 1 else lhs[0]
            term = dot(lhs, w1_mat[pair * 256 : pair * 256 + lhs.shape[1], :])
            acc = term if acc is None else acc + term
        act = jnp.maximum(acc + b1_loc[...], 0.0).reshape(10, rows, C2)
        ok = inside[:, top : top + rows] > 0.0
        real = [jnp.where(ok, act[:, :, half * 128 : half * 128 + 128], 0.0) for half in range(2)]
        for half in range(2):
            part = slice(half * 128, half * 128 + 128)
            ys0[:, top : top + rows, part] = real[half].astype(jnp.bfloat16)
            if before is None:
                ys8[:, 0 : rows - 16, part] = real[half][:, 8 : rows - 8].astype(jnp.bfloat16)
            else:
                shifted = jnp.concatenate([before[half], real[half][:, 0 : rows - 8]], axis=1)
                ys8[:, top - 16 : top + rows - 16, part] = shifted.astype(jnp.bfloat16)
        before = [r[:, rows - 8 :] for r in real]

    for blk in range(3):
        conv_two(blk, ys0, ys8, w2_mat, b2_loc, res.at[blk], out_ref)

    drain(r_w, send_w)
    drain(s_x, send_x)
    swap.wait_send()


def conv_two(blk, ys0, ys8, w2_mat, b2_ref, res, out_ref):
    acc = None
    for tap in range(9):
        dh, dw = tap // 3, tap % 3
        src = ys8 if dh == 1 else ys0
        at = blk * 32 + (16 if dh == 2 else 0)
        term = dot(src[dw : dw + 8, at : at + 32].reshape(256, C2), w2_mat[dh, dw])
        acc = term if acc is None else acc + term
    full = acc + b2_ref[...]
    for w in range(8):
        for half in range(2):
            res[half, w * OUT_COL : w * OUT_COL + 32] = full[w * 32 : w * 32 + 32, half * 128 : half * 128 + 128]
    for h in range(4):
        for n in range(8):
            for half in range(2):
                rows = res.at[half][pl.ds(h * 8 + n, 8, stride=OUT_COL), :]
                out_ref[n, (blk * 4) % out_ref.shape[1] + h, :, half * 128 : half * 128 + 128] = rows


def kernel_two(out_a, ys0, ys8, w2_mat, b2_ref, out_hbm, out_b, res, sem):
    put_a = pltpu.make_async_copy(out_a, out_hbm.at[:, 0:12], sem.at[0])
    put_a.start()
    conv_two(3, ys0, ys8, w2_mat, b2_ref, res, out_b)
    put_b = pltpu.make_async_copy(out_b, out_hbm.at[:, 12:16], sem.at[1])
    put_b.start()
    put_a.wait()
    put_b.wait()


def solution(mesh):
    def run_local(x_in, w_conv1, b_conv1, w_conv2, b_conv2):
        bf, f32 = jnp.bfloat16, jnp.float32
        vmem = pl.BlockSpec(memory_space=pltpu.VMEM)
        hbm = pl.BlockSpec(memory_space=pltpu.HBM)
        dma = pltpu.SemaphoreType.DMA
        operands = (x_in.reshape(x_in.shape[:3]), w_conv1.reshape(3, 3, C2), b_conv1.reshape(1, C2), w_conv2, b_conv2.reshape(1, C2))
        out_a, ys0, ys8, w2 = pl.pallas_call(
            kernel,
            name="conv_pair",
            out_shape=[
                jax.ShapeDtypeStruct((8, 12, 8, C2), f32),
                jax.ShapeDtypeStruct((10, MID_COL, C2), bf),
                jax.ShapeDtypeStruct((10, 128, C2), bf),
                jax.ShapeDtypeStruct((3, 3, C2, C2), bf),
            ],
            in_specs=[hbm] * 5,
            out_specs=[vmem] * 4,
            scratch_shapes=[
                pltpu.VMEM((8, 128, 128), bf),
                pltpu.VMEM((3, 3, C2), bf),
                pltpu.VMEM((1, C2), f32),
                pltpu.VMEM((1, C2), f32),
                pltpu.VMEM((128, 1024), bf),
                pltpu.VMEM((1024, 2048), bf),
                pltpu.VMEM((256, 1024), bf),
                pltpu.VMEM((256, 256), bf),
                pltpu.VMEM((2, 5, 2, 128), bf),
                pltpu.VMEM((N_DEV, 2, 8, 128), bf),
                pltpu.VMEM((N_DEV, 5, 2, 128), bf),
                pltpu.VMEM((N_DEV, 5, 2, 128), bf),
                pltpu.VMEM((N_DEV, 2, 8, 128), bf),
                pltpu.VMEM((9 * C1, C2), bf),
                pltpu.VMEM((2, N_DEV * 8, 128), f32),
                pltpu.VMEM((3, 128, 128), f32),
                pltpu.VMEM((12, COL, C1), bf),
                pltpu.VMEM((12, MID_COL, C1), bf),
                pltpu.VMEM((10, MID_COL, 128), f32),
                pltpu.VMEM((3, 2, 8 * OUT_COL, 128), f32),
                pltpu.SemaphoreType.REGULAR, dma, dma, pltpu.SemaphoreType.DMA((2,)), dma,
                dma, dma, dma, dma, dma, dma,
            ],
            compiler_params=pltpu.CompilerParams(collective_id=0, has_side_effects=True, vmem_limit_bytes=24 << 20),
        )(*(pltpu.with_memory_space_constraint(a, pltpu.HBM) for a in operands))
        return pl.pallas_call(
            kernel_two,
            name="conv_last",
            out_shape=jax.ShapeDtypeStruct((8, 16, 8, C2), f32),
            in_specs=[vmem] * 5,
            out_specs=hbm,
            scratch_shapes=[pltpu.VMEM((8, 4, 8, C2), f32), pltpu.VMEM((2, 8 * OUT_COL, 128), f32), pltpu.SemaphoreType.DMA((2,))],
            compiler_params=pltpu.CompilerParams(vmem_limit_bytes=24 << 20),
        )(out_a, ys0, ys8, w2, operands[-1])

    return jax.shard_map(
        run_local,
        mesh=mesh,
        in_specs=(P("data", None, None, GROUP_AXES), P(None, None, GROUP_AXES, None), P(), P(), P()),
        out_specs=P("data", "model", "cols", None),
        check_vma=False,
    )
```

time: 26.3 us -> 22.7 us (0.86)
  Pallas kernels: 26.2 us -> 22.6 us
    pallas_call x2, Pallas kernels: 26.2 us -> 22.6 us  [the longest x1 21.3 us: run_local(): pl.pallas_call(kernel, name='conv_pair', out_shape=[jax.ShapeDtypeStruct(...]
where the time goes in v4:
time: 22.7 us; the launch traced here: 22.6 us
  Pallas kernels  22.6 us (100%)
    pallas_call x1, Pallas kernels, run_local(): pl.pallas_call(kernel, name='conv_pair', out_shape=[jax.ShapeDtypeStruct(...  21.3 us
    pallas_call x1, Pallas kernels, run_local(): pl.pallas_call(kernel_two, name='conv_last', out_shape=jax.ShapeDtypeStru...  1.26 us

profile of v4, /device:TPU:1, one launch (start us, length us, event | category | flops | bytes accessed | tf_op | source)
XLA Modules:
  0.0 22.6 jit_solution(11579442946311454344)
XLA Ops:
  0.0 0.0 copy-start
  0.0 21.3 %conv_pair.1 = (f32[8,12,8,256]{3,2,1,0:T(8,128)S(1)}, bf16[10,144,256]{2,1,0:T(8,128)(2,1)S(1)}, bf16[10,128,256]{2,1,0:T(8,128)(2,1)S(1)}, bf16[3,3,256,256]{3,2,1,0:T(8,128)(2,1)S(1)}) custom-call(bf16[8,128,128]{2,1,0:T(8,128)(2,1)} %bitcast.6, bf16[3,3,256]{2,1,0:T(4,128)(2,1)} %bitcast.7, f32[1,256]{1,0:T(1,128)} %bitcast.8, ...), custom_call_target="tpu_custom_call" | custom-call | tf_op jit(solution)/shard_map/conv_pair/pallas_call | solution.py:286
  21.3 0.0 copy-done
  21.4 1.3 %conv_last.1 = f32[8,16,8,256]{3,2,1,0:T(8,128)} custom-call(f32[8,12,8,256]{3,2,1,0:T(8,128)S(1)} %get-tuple-element.9.out_a, bf16[10,144,256]{2,1,0:T(8,128)(2,1)S(1)} %get-tuple-element.10.ys0, bf16[10,128,256]{2,1,0:T(8,128)(2,1)S(1)} %get-tuple-element.11.ys8, bf16[3,3,256,256]{3,2,1,0:T(8,128)(2,1)S(1)} %get-tuple-element.12.w2_mat, f32[1,256]{1,0:T(1,128)S(1)} %bitcast.5), custom_call_target="tpu_custom_call" | custom-call | tf_op jit(solution)/shard_map/conv_last/pallas_call | solution.py:323
Async XLA Ops:
  0.0 21.3 %copy-start = (f32[256]{0:T(256)S(1)}, f32[256]{0:T(256)}, u32[]{:S(2)}) copy-start(f32[256]{0:T(256)} %param.9) | copy-start | bytes 3076

commit v5 on v4

--- a/solution.py
+++ b/solution.py
@@ -29,14 +29,15 @@
 def send_order():
     def key(msg):
         window, dx, dy, z, dk = msg
-        return (z // 2, 11 * (z == 1) + 100 * window - 10 * HOPS[dy] + 0.1 * (3, 1, 0, 2)[dx] + 0.01 * dk)
+        return (z > 0, 11 * (z > 1) + 100 * window - 10 * HOPS[dy] + 0.1 * (3, 1, 0, 2)[dx] + 0.01 * dk)
 
     return sorted(((w, dx, dy, z, dk) for w in range(2) for dx in range(4) for dy in range(4) for z in range(4) for dk in range(2)), key=key)
 
 
 GREET_ORDER = greet_order()
 SEND_ORDER = send_order()
-EARLY = ((0,), (2, 3))
+SPLIT = 1
+EARLY = {32: 0, 160: 1}
 
 
 def dot(a, b):
@@ -69,7 +70,7 @@
     zs = [((my_z + dz) % 4) * 4 for dz in range(4)]
 
     barrier = pltpu.get_barrier_semaphore()
-    part = my_z // 2
+    part = (my_z + 4 - SPLIT) // 4
     partner = {"model": m + 1 - 2 * core, "cols": c}
     for dx, dy, dz in GREET_ORDER:
         to = {"model": ((m // 2 + dx) % 4) * 2 + part, "cols": zs[dz] + ys[dy]}
@@ -79,7 +80,7 @@
     def hear(which):
         @pl.when(core == which)
         def _():
-            pl.semaphore_wait(barrier, 63 + 2 * ((core + part) % 2))
+            pl.semaphore_wait(barrier, (SPLIT * 32, 128 - SPLIT * 32)[which] - 1 + 2 * ((core + part) % 2))
             pl.semaphore_signal(heard, inc=1, device_id=partner, device_id_type=MESH)
 
         @pl.when(core != which)
@@ -141,14 +142,13 @@
                                      device_id={"model": pm, "cols": pc}, device_id_type=MESH).start()
 
     for step, (window, dx, dy, z, dk) in enumerate(SEND_ORDER):
-        if step % N_DEV == 0:
-            hear(step // N_DEV)
-        if window and SEND_ORDER[step - 1][0] == 0:
-            for first_z in EARLY[step // N_DEV]:
-                for k in (1, 0):
-                    def send_early(pm=k, pc=first_z * 4):
-                        send(s_x.at[pm * N_COLS + pc], r_x.at[me], send_x, recv_x, pm, pc)
-                    pl.when(me != k * N_COLS + first_z * 4)(send_early)
+        if step in (0, SPLIT * 64):
+            hear(min(step, 1))
+        if step in EARLY:
+            for k in (1, 0):
+                def send_early(pm=k, pc=EARLY[step] * 4):
+                    send(s_x.at[pm * N_COLS + pc], r_x.at[me], send_x, recv_x, pm, pc)
+                pl.when(me != k * N_COLS + EARLY[step] * 4)(send_early)
         pm, pc = models[dx][dk], z * 4 + ys[dy]
 
         def send_one(window=window, pm=pm, pc=pc, pk=cores[dk]):
@@ -157,7 +157,7 @@
             else:
                 send(s_w.at[pk], r_w.at[me], send_w, recv_w, pm, pc)
 
-        if window and z in EARLY[z // 2]:
+        if window and z in EARLY.values():
             sent = models[dx][0] // 2 + ys[dy] == 0
             skip = sent | (my_z == z) if dx == dy == dk == 0 else sent
             pl.when(jnp.logical_not(skip))(send_one)

time: 22.7 us -> 21.8 us (0.960)
  the two profiles are of different devices: /device:TPU:1 before, /device:TPU:65 now
where the time goes in v5:
time: 21.8 us; the launch traced here: 21.7 us
  Pallas kernels  21.7 us (100%)
    pallas_call x1, Pallas kernels, run_local(): pl.pallas_call(kernel, name='conv_pair', out_shape=[jax.ShapeDtypeStruct(...  20.4 us
    pallas_call x1, Pallas kernels, run_local(): pl.pallas_call(kernel_two, name='conv_last', out_shape=jax.ShapeDtypeStru...  1.27 us

profile of v5, /device:TPU:65, one launch (start us, length us, event | category | flops | bytes accessed | tf_op | source)
XLA Modules:
  0.0 21.7 jit_solution(13814872847371499229)
XLA Ops:
  0.0 0.0 copy-start
  0.0 20.4 %conv_pair.1 = (f32[8,12,8,256]{3,2,1,0:T(8,128)S(1)}, bf16[10,144,256]{2,1,0:T(8,128)(2,1)S(1)}, bf16[10,128,256]{2,1,0:T(8,128)(2,1)S(1)}, bf16[3,3,256,256]{3,2,1,0:T(8,128)(2,1)S(1)}) custom-call(bf16[8,128,128]{2,1,0:T(8,128)(2,1)} %bitcast.6, bf16[3,3,256]{2,1,0:T(4,128)(2,1)} %bitcast.7, f32[1,256]{1,0:T(1,128)} %bitcast.8, ...), custom_call_target="tpu_custom_call" | custom-call | tf_op jit(solution)/shard_map/conv_pair/pallas_call | solution.py:286
  20.4 0.0 copy-done
  20.4 1.3 %conv_last.1 = f32[8,16,8,256]{3,2,1,0:T(8,128)} custom-call(f32[8,12,8,256]{3,2,1,0:T(8,128)S(1)} %get-tuple-element.9.out_a, bf16[10,144,256]{2,1,0:T(8,128)(2,1)S(1)} %get-tuple-element.10.ys0, bf16[10,128,256]{2,1,0:T(8,128)(2,1)S(1)} %get-tuple-element.11.ys8, bf16[3,3,256,256]{3,2,1,0:T(8,128)(2,1)S(1)} %get-tuple-element.12.w2_mat, f32[1,256]{1,0:T(1,128)S(1)} %bitcast.5), custom_call_target="tpu_custom_call" | custom-call | tf_op jit(solution)/shard_map/conv_last/pallas_call | solution.py:323
Async XLA Ops:
  0.0 20.4 %copy-start = (f32[256]{0:T(256)S(1)}, f32[256]{0:T(256)}, u32[]{:S(2)}) copy-start(f32[256]{0:T(256)} %param.9) | copy-start | bytes 3076

commit v6 on v4

--- a/solution.py
+++ b/solution.py
@@ -16,6 +16,8 @@
 COL = 160
 MID_COL = 144
 OUT_COL = 40
+BLOCKS = ((0, 4), (4, 4), (8, 4), (12, 2))
+LAST = 14
 C1 = 128
 C2 = 256
 HOPS = (0, 1, 2, 1)
@@ -26,17 +28,19 @@
     return sorted(shifts, key=lambda s: (-HOPS[s[1]] - HOPS[s[2]], -HOPS[s[0]]))
 
 
-def send_order():
-    def key(msg):
-        window, dx, dy, z, dk = msg
-        return (z // 2, 11 * (z == 1) + 100 * window - 10 * HOPS[dy] + 0.1 * (3, 1, 0, 2)[dx] + 0.01 * dk)
-
-    return sorted(((w, dx, dy, z, dk) for w in range(2) for dx in range(4) for dy in range(4) for z in range(4) for dk in range(2)), key=key)
-
-
 GREET_ORDER = greet_order()
-SEND_ORDER = send_order()
-EARLY = ((0,), (2, 3))
+SEND_ORDER = ((
+    16, 112, 80, 48, 8, 104, 24, 72, 120, 40, 88, 56, 0, 96, 64, 32, 145, 144, 241, 240, 209, 208, 177, 176,
+    137, 136, 233, 232, 153, 152, 201, 249, 200, 248, 169, 168, 217, 216, 185, 184, 129, 128, 225, 224, 193, 192, 161, 160,
+), (
+    18, 114, 82, 50, 10, 106, 26, 20, 22, 74, 122, 42, 116, 118, 90, 58, 84, 86, 52, 54, 12, 14, 2, 108,
+    110, 28, 30, 98, 76, 78, 124, 126, 44, 46, 66, 34, 92, 94, 60, 62, 4, 6, 100, 102, 68, 70, 36, 38,
+    147, 146, 243, 242, 211, 210, 179, 178, 139, 138, 235, 234, 155, 154, 149, 151, 203, 251, 148, 150, 202, 250, 171, 170,
+    245, 247, 244, 246, 219, 218, 187, 186, 213, 215, 212, 214, 181, 183, 180, 182, 141, 143, 140, 142, 131, 237, 239, 130,
+    236, 238, 157, 159, 227, 156, 158, 226, 205, 207, 253, 255, 204, 206, 252, 254, 173, 175, 172, 174, 195, 194, 163, 162,
+    221, 223, 220, 222, 189, 191, 188, 190, 133, 135, 132, 134, 229, 231, 228, 230, 197, 199, 196, 198, 165, 167, 164, 166,
+))
+EARLY = ({}, {})
 
 
 def dot(a, b):
@@ -49,8 +53,9 @@
            heard, sem_x, sem_w1, sem_b, sem_w2, send_w, send_x, send_d, recv_w, recv_x, recv_d):
     m = lax.axis_index("model")
     c = lax.axis_index("cols")
-    me = m * N_COLS + c
     core = m % 2
+    chip = m // 2 * N_COLS + c
+    me = core * 64 + chip
 
     get_x = pltpu.make_async_copy(x_hbm, x_loc, sem_x)
     get_x.start()
@@ -69,7 +74,7 @@
     zs = [((my_z + dz) % 4) * 4 for dz in range(4)]
 
     barrier = pltpu.get_barrier_semaphore()
-    part = my_z // 2
+    part = (my_z + 3) // 4
     partner = {"model": m + 1 - 2 * core, "cols": c}
     for dx, dy, dz in GREET_ORDER:
         to = {"model": ((m // 2 + dx) % 4) * 2 + part, "cols": zs[dz] + ys[dy]}
@@ -79,7 +84,7 @@
     def hear(which):
         @pl.when(core == which)
         def _():
-            pl.semaphore_wait(barrier, 63 + 2 * ((core + part) % 2))
+            pl.semaphore_wait(barrier, (32, 96)[which] - 1 + 2 * ((core + part) % 2))
             pl.semaphore_signal(heard, inc=1, device_id=partner, device_id_type=MESH)
 
         @pl.when(core != which)
@@ -107,12 +112,8 @@
     border = (s_id >= 12) & (s_id < 15) & (k_id >= 128 + jnp.maximum(from_col, 0)) & (k_id < 132 + from_col)
     place[...] = jnp.where(main | border, 1.0, 0.0).astype(jnp.bfloat16)
     get_w1.wait()
-    for k in range(2):
-        for j in range(4):
-            tap = 4 * k + j
-            s_w[k, j] = jnp.concatenate([w1_loc[tap // 3, tap % 3 : tap % 3 + 1, half * 128 : half * 128 + 128] for half in range(2)])
-        last = w1_loc[2, 2:3, k * 128 : k * 128 + 128]
-        s_w[k, 4] = jnp.concatenate([last, jnp.zeros_like(last)])
+    for tap in range(9):
+        s_w[tap] = jnp.concatenate([w1_loc[tap // 3, tap % 3 : tap % 3 + 1, half * 128 : half * 128 + 128] for half in range(2)])
 
     get_x.wait()
     for n in range(8):
@@ -140,54 +141,52 @@
         pltpu.make_async_remote_copy(src_ref=src, dst_ref=dst, send_sem=send_sem, recv_sem=recv_sem,
                                      device_id={"model": pm, "cols": pc}, device_id_type=MESH).start()
 
-    for step, (window, dx, dy, z, dk) in enumerate(SEND_ORDER):
-        if step % N_DEV == 0:
-            hear(step // N_DEV)
-        if window and SEND_ORDER[step - 1][0] == 0:
-            for first_z in EARLY[step // N_DEV]:
+    early_zs = {z for early in EARLY for layers in early.values() for z in layers}
+    for which, order in enumerate(SEND_ORDER):
+        hear(which)
+        for pos, msg in enumerate(order):
+            window, dx, dy, z, dk = msg // 128, msg // 32 % 4, msg // 8 % 4, msg // 2 % 4, msg % 2
+            for ez in EARLY[which].get(pos, ()):
                 for k in (1, 0):
-                    def send_early(pm=k, pc=first_z * 4):
+                    def send_early(pm=k, pc=ez * 4):
                         send(s_x.at[pm * N_COLS + pc], r_x.at[me], send_x, recv_x, pm, pc)
-                    pl.when(me != k * N_COLS + first_z * 4)(send_early)
-        pm, pc = models[dx][dk], z * 4 + ys[dy]
-
-        def send_one(window=window, pm=pm, pc=pc, pk=cores[dk]):
-            if window:
-                send(s_x.at[pm * N_COLS + pc], r_x.at[me], send_x, recv_x, pm, pc)
+                    pl.when((m != k) | (c != ez * 4))(send_early)
+            pm, pc = models[dx][dk], z * 4 + ys[dy]
+
+            def send_one(window=window, pm=pm, pc=pc):
+                if window:
+                    send(s_x.at[pm * N_COLS + pc], r_x.at[me], send_x, recv_x, pm, pc)
+                else:
+                    send(s_w, r_w.at[chip], send_w, recv_w, pm, pc)
+
+            conds = []
+            if dx == dy == dk == 0:
+                conds.append(my_z != z)
+            if window and z in early_zs:
+                conds.append(models[dx][0] // 2 + ys[dy] != 0)
+            if conds:
+                pl.when(functools.reduce(lambda p, q: p & q, conds))(send_one)
             else:
-                send(s_w.at[pk], r_w.at[me], send_w, recv_w, pm, pc)
-
-        if window and z in EARLY[z // 2]:
-            sent = models[dx][0] // 2 + ys[dy] == 0
-            skip = sent | (my_z == z) if dx == dy == dk == 0 else sent
-            pl.when(jnp.logical_not(skip))(send_one)
-        elif dx == dy == dk == 0:
-            pl.when(my_z != z)(send_one)
-        else:
-            send_one()
-    r_w[pl.ds(me, 1)] = s_w[pl.ds(core, 1)]
-    r_x[pl.ds(me, 1)] = s_x[pl.ds(me, 1)]
+                send_one()
+    r_w[pl.ds(chip, 1)] = s_w[...].reshape(1, 9, 2, 128)
+    r_x[pl.ds(me, 1)] = s_x[pl.ds(m * N_COLS + c, 1)]
 
     at_row = m * 16 - 1 + lax.broadcasted_iota(jnp.int32, (10, MID_COL, 128), 1) // 8
     at_col = c * 8 - 1 + lax.broadcasted_iota(jnp.int32, (10, MID_COL, 128), 0)
     inside[...] = jnp.where((at_row >= 0) & (at_row < 128) & (at_col >= 0) & (at_col < 128), 1.0, 0.0)
 
-    def drain(ref, sem):
-        part = ref.at[pl.ds(0, N_DEV - 1)]
+    def drain(ref, count, sem):
+        part = ref.at[pl.ds(0, count)]
         pltpu.make_async_copy(part, part, sem).wait()
 
     def unpack_w(ref, k):
-        for j in range(5):
-            tmp[0, 0 : 2 * N_DEV] = ref[:, j].astype(jnp.float32).reshape(N_DEV * 2, 128)
-            for half in range(2 if j < 4 else 1):
-                rows = tmp.at[0][pl.ds(half, N_DEV, stride=2), :].astype(jnp.bfloat16)
-                if j < 4:
-                    at = pl.multiple_of((4 * k + j) * C1, C1)
-                    w1_mat[pl.ds(at, C1), half * 128 : half * 128 + 128] = rows
-                else:
-                    w1_mat[8 * C1 : 9 * C1, pl.ds(pl.multiple_of(k * 128, 128), 128)] = rows
-
-    drain(r_w, recv_w)
+        for tap in range(9):
+            tmp[0, 0:N_DEV] = ref[:, tap].astype(jnp.float32).reshape(N_DEV, 128)
+            at = pl.multiple_of(tap * C1 + k * 64, 64)
+            for half in range(2):
+                w1_mat[pl.ds(at, 64), half * 128 : half * 128 + 128] = tmp.at[0][pl.ds(half, 64, stride=2), :].astype(jnp.bfloat16)
+
+    drain(r_w, 63, recv_w)
     swap = pltpu.make_async_remote_copy(src_ref=r_w, dst_ref=r_w2, send_sem=send_d, recv_sem=recv_d,
                                         device_id=partner, device_id_type=MESH)
     swap.start()
@@ -198,7 +197,7 @@
         get.wait()
     get_w2.wait()
 
-    drain(r_x, recv_x)
+    drain(r_x, N_DEV - 1, recv_x)
     for half in range(2):
         tmp[half] = r_x[:, half].astype(jnp.float32).reshape(N_DEV * 8, 128)
 
@@ -239,38 +238,43 @@
                 ys8[:, top - 16 : top + rows - 16, part] = shifted.astype(jnp.bfloat16)
         before = [r[:, rows - 8 :] for r in real]
 
-    for blk in range(3):
-        conv_two(blk, ys0, ys8, w2_mat, b2_loc, res.at[blk], out_ref)
-
-    drain(r_w, send_w)
-    drain(s_x, send_x)
+    for i, (top, rows) in enumerate(BLOCKS):
+        conv_two(top, rows, 1, ys0, ys8, w2_mat, b2_loc, res.at[i], out_ref)
+
+    drain(r_w, 63, send_w)
+    drain(s_x, N_DEV - 1, send_x)
     swap.wait_send()
 
 
-def conv_two(blk, ys0, ys8, w2_mat, b2_ref, res, out_ref):
-    acc = None
-    for tap in range(9):
-        dh, dw = tap // 3, tap % 3
-        src = ys8 if dh == 1 else ys0
-        at = blk * 32 + (16 if dh == 2 else 0)
-        term = dot(src[dw : dw + 8, at : at + 32].reshape(256, C2), w2_mat[dh, dw])
-        acc = term if acc is None else acc + term
-    full = acc + b2_ref[...]
-    for w in range(8):
-        for half in range(2):
-            res[half, w * OUT_COL : w * OUT_COL + 32] = full[w * 32 : w * 32 + 32, half * 128 : half * 128 + 128]
-    for h in range(4):
+def conv_two(top, rows, parts, ys0, ys8, w2_mat, b2_ref, res, out_ref):
+    cols = 8 // parts
+    size = rows * 8
+    for part in range(parts):
+        acc = None
+        for tap in range(9):
+            dh, dw = tap // 3, tap % 3
+            src = ys8 if dh == 1 else ys0
+            at = top * 8 + (16 if dh == 2 else 0)
+            lo = dw + part * cols
+            term = dot(src[lo : lo + cols, at : at + size].reshape(cols * size, C2), w2_mat[dh, dw])
+            acc = term if acc is None else acc + term
+        full = acc + b2_ref[...]
+        for w in range(cols):
+            for half in range(2):
+                to = (part * cols + w) * (size + 8)
+                res[half, to : to + size] = full[w * size : w * size + size, half * 128 : half * 128 + 128]
+    for h in range(rows):
         for n in range(8):
             for half in range(2):
-                rows = res.at[half][pl.ds(h * 8 + n, 8, stride=OUT_COL), :]
-                out_ref[n, (blk * 4) % out_ref.shape[1] + h, :, half * 128 : half * 128 + 128] = rows
+                vals = res.at[half][pl.ds(h * 8 + n, 8, stride=size + 8), :]
+                out_ref[n, top % out_ref.shape[1] + h, :, half * 128 : half * 128 + 128] = vals
 
 
 def kernel_two(out_a, ys0, ys8, w2_mat, b2_ref, out_hbm, out_b, res, sem):
-    put_a = pltpu.make_async_copy(out_a, out_hbm.at[:, 0:12], sem.at[0])
+    put_a = pltpu.make_async_copy(out_a, out_hbm.at[:, 0:LAST], sem.at[0])
     put_a.start()
-    conv_two(3, ys0, ys8, w2_mat, b2_ref, res, out_b)
-    put_b = pltpu.make_async_copy(out_b, out_hbm.at[:, 12:16], sem.at[1])
+    conv_two(LAST, 16 - LAST, 1, ys0, ys8, w2_mat, b2_ref, res, out_b)
+    put_b = pltpu.make_async_copy(out_b, out_hbm.at[:, LAST:16], sem.at[1])
     put_b.start()
     put_a.wait()
     put_b.wait()
@@ -287,7 +291,7 @@
             kernel,
             name="conv_pair",
             out_shape=[
-                jax.ShapeDtypeStruct((8, 12, 8, C2), f32),
+                jax.ShapeDtypeStruct((8, LAST, 8, C2), f32),
                 jax.ShapeDtypeStruct((10, MID_COL, C2), bf),
                 jax.ShapeDtypeStruct((10, 128, C2), bf),
                 jax.ShapeDtypeStruct((3, 3, C2, C2), bf),
@@ -303,10 +307,10 @@
                 pltpu.VMEM((1024, 2048), bf),
                 pltpu.VMEM((256, 1024), bf),
                 pltpu.VMEM((256, 256), bf),
-                pltpu.VMEM((2, 5, 2, 128), bf),
+                pltpu.VMEM((9, 2, 128), bf),
                 pltpu.VMEM((N_DEV, 2, 8, 128), bf),
-                pltpu.VMEM((N_DEV, 5, 2, 128), bf),
-                pltpu.VMEM((N_DEV, 5, 2, 128), bf),
+                pltpu.VMEM((64, 9, 2, 128), bf),
+                pltpu.VMEM((64, 9, 2, 128), bf),
                 pltpu.VMEM((N_DEV, 2, 8, 128), bf),
                 pltpu.VMEM((9 * C1, C2), bf),
                 pltpu.VMEM((2, N_DEV * 8, 128), f32),
@@ -314,7 +318,7 @@
                 pltpu.VMEM((12, COL, C1), bf),
                 pltpu.VMEM((12, MID_COL, C1), bf),
                 pltpu.VMEM((10, MID_COL, 128), f32),
-                pltpu.VMEM((3, 2, 8 * OUT_COL, 128), f32),
+                pltpu.VMEM((len(BLOCKS), 2, 8 * OUT_COL, 128), f32),
                 pltpu.SemaphoreType.REGULAR, dma, dma, pltpu.SemaphoreType.DMA((2,)), dma,
                 dma, dma, dma, dma, dma, dma,
             ],
@@ -326,7 +330,7 @@
             out_shape=jax.ShapeDtypeStruct((8, 16, 8, C2), f32),
             in_specs=[vmem] * 5,
             out_specs=hbm,
-            scratch_shapes=[pltpu.VMEM((8, 4, 8, C2), f32), pltpu.VMEM((2, 8 * OUT_COL, 128), f32), pltpu.SemaphoreType.DMA((2,))],
+            scratch_shapes=[pltpu.VMEM((8, 16 - LAST, 8, C2), f32), pltpu.VMEM((2, 8 * OUT_COL, 128), f32), pltpu.SemaphoreType.DMA((2,))],
             compiler_params=pltpu.CompilerParams(vmem_limit_bytes=24 << 20),
         )(out_a, ys0, ys8, w2, operands[-1])
 

time: 22.7 us -> 21.6 us (0.952)
  the two profiles are of different devices: /device:TPU:1 before, /device:TPU:32 now
where the time goes in v6:
time: 21.6 us; the launch traced here: 21.5 us
  Pallas kernels  21.4 us (99%)
    pallas_call x1, Pallas kernels, run_local(): pl.pallas_call(kernel, name='conv_pair', out_shape=[jax.ShapeDtypeStruct(...  20.4 us
    pallas_call x1, Pallas kernels, run_local(): pl.pallas_call(kernel_two, name='conv_last', out_shape=jax.ShapeDtypeStru...  1.03 us

profile of v6, /device:TPU:32, one launch (start us, length us, event | category | flops | bytes accessed | tf_op | source)
XLA Modules:
  0.0 21.5 jit_solution(7344267458791241579)
XLA Ops:
  0.0 0.0 copy-start
  0.0 20.4 %conv_pair.1 = (f32[8,14,8,256]{3,2,1,0:T(8,128)S(1)}, bf16[10,144,256]{2,1,0:T(8,128)(2,1)S(1)}, bf16[10,128,256]{2,1,0:T(8,128)(2,1)S(1)}, bf16[3,3,256,256]{3,2,1,0:T(8,128)(2,1)S(1)}) custom-call(bf16[8,128,128]{2,1,0:T(8,128)(2,1)} %bitcast.6, bf16[3,3,256]{2,1,0:T(4,128)(2,1)} %bitcast.7, f32[1,256]{1,0:T(1,128)} %bitcast.8, ...), custom_call_target="tpu_custom_call" | custom-call | tf_op jit(solution)/shard_map/conv_pair/pallas_call | solution.py:290
  20.4 0.0 copy-done
  20.4 1.0 %conv_last.1 = f32[8,16,8,256]{3,2,1,0:T(8,128)} custom-call(f32[8,14,8,256]{3,2,1,0:T(8,128)S(1)} %get-tuple-element.9.out_a, bf16[10,144,256]{2,1,0:T(8,128)(2,1)S(1)} %get-tuple-element.10.ys0, bf16[10,128,256]{2,1,0:T(8,128)(2,1)S(1)} %get-tuple-element.11.ys8, bf16[3,3,256,256]{3,2,1,0:T(8,128)(2,1)S(1)} %get-tuple-element.12.w2_mat, f32[1,256]{1,0:T(1,128)S(1)} %bitcast.5), custom_call_target="tpu_custom_call" | custom-call | tf_op jit(solution)/shard_map/conv_last/pallas_call | solution.py:327
Async XLA Ops:
  0.0 20.4 %copy-start = (f32[256]{0:T(256)S(1)}, f32[256]{0:T(256)}, u32[]{:S(2)}) copy-start(f32[256]{0:T(256)} %param.9) | copy-start | bytes 3076

commit v7 on v6

--- a/solution.py
+++ b/solution.py
@@ -29,18 +29,27 @@
 
 
 GREET_ORDER = greet_order()
-SEND_ORDER = ((
-    16, 112, 80, 48, 8, 104, 24, 72, 120, 40, 88, 56, 0, 96, 64, 32, 145, 144, 241, 240, 209, 208, 177, 176,
-    137, 136, 233, 232, 153, 152, 201, 249, 200, 248, 169, 168, 217, 216, 185, 184, 129, 128, 225, 224, 193, 192, 161, 160,
-), (
-    18, 114, 82, 50, 10, 106, 26, 20, 22, 74, 122, 42, 116, 118, 90, 58, 84, 86, 52, 54, 12, 14, 2, 108,
-    110, 28, 30, 98, 76, 78, 124, 126, 44, 46, 66, 34, 92, 94, 60, 62, 4, 6, 100, 102, 68, 70, 36, 38,
-    147, 146, 243, 242, 211, 210, 179, 178, 139, 138, 235, 234, 155, 154, 149, 151, 203, 251, 148, 150, 202, 250, 171, 170,
-    245, 247, 244, 246, 219, 218, 187, 186, 213, 215, 212, 214, 181, 183, 180, 182, 141, 143, 140, 142, 131, 237, 239, 130,
-    236, 238, 157, 159, 227, 156, 158, 226, 205, 207, 253, 255, 204, 206, 252, 254, 173, 175, 172, 174, 195, 194, 163, 162,
-    221, 223, 220, 222, 189, 191, 188, 190, 133, 135, 132, 134, 229, 231, 228, 230, 197, 199, 196, 198, 165, 167, 164, 166,
-))
-EARLY = ({}, {})
+LATER_Z = ((0, 6, 14, 11), (100, 100, 108, 105))
+LATER_Y = ((20, 6, 0, 10), (20, 8, 0, 12))
+LATER_X = ((-3, 0, -1, -2), (0.0, 0.31000000000000005, 0.30000000000000004, 0.1))
+LATER_CORE = -0.01
+MIX = (0, 1, 1, 1, 1, 1)
+EARLY = (1,)
+
+
+def send_order():
+    def key(msg):
+        window, dx, dy, z, dk = msg
+        mix = (MIX[1] * window + MIX[2] * dx + MIX[3] * dy + MIX[4] * z) * (MIX[5] + dk) % 17
+        return LATER_Z[window][z] + LATER_Y[window][dy] + LATER_X[window][dx] + LATER_CORE * dk + MIX[0] * mix
+
+    windows = [(1, dx, dy, z, dk) for dx in range(4) for dy in range(4) for z in range(4) for dk in range(2)]
+    weights = [(0, dx, dy, z, 0) for dx in range(4) for dy in range(4) for z in range(4)]
+    order = sorted(weights + windows, key=key)
+    return [m for m in order if m[3] == 0], [m for m in order if m[3] > 0]
+
+
+SEND_ORDER = send_order()
 
 
 def dot(a, b):
@@ -141,16 +150,16 @@
         pltpu.make_async_remote_copy(src_ref=src, dst_ref=dst, send_sem=send_sem, recv_sem=recv_sem,
                                      device_id={"model": pm, "cols": pc}, device_id_type=MESH).start()
 
-    early_zs = {z for early in EARLY for layers in early.values() for z in layers}
     for which, order in enumerate(SEND_ORDER):
         hear(which)
-        for pos, msg in enumerate(order):
-            window, dx, dy, z, dk = msg // 128, msg // 32 % 4, msg // 8 % 4, msg // 2 % 4, msg % 2
-            for ez in EARLY[which].get(pos, ()):
+        served = set()
+        for window, dx, dy, z, dk in order:
+            if window and z in EARLY and z not in served:
+                served.add(z)
                 for k in (1, 0):
-                    def send_early(pm=k, pc=ez * 4):
+                    def send_early(pm=k, pc=z * 4):
                         send(s_x.at[pm * N_COLS + pc], r_x.at[me], send_x, recv_x, pm, pc)
-                    pl.when((m != k) | (c != ez * 4))(send_early)
+                    pl.when((m != k) | (c != z * 4))(send_early)
             pm, pc = models[dx][dk], z * 4 + ys[dy]
 
             def send_one(window=window, pm=pm, pc=pc):
@@ -162,7 +171,7 @@
             conds = []
             if dx == dy == dk == 0:
                 conds.append(my_z != z)
-            if window and z in early_zs:
+            if window and z in EARLY:
                 conds.append(models[dx][0] // 2 + ys[dy] != 0)
             if conds:
                 pl.when(functools.reduce(lambda p, q: p & q, conds))(send_one)

time: 21.6 us -> 21.2 us (0.981)
  Pallas kernels: 21.4 us -> 21.1 us
    pallas_call x1, Pallas kernels: 20.4 us -> 20.1 us  [run_local(): pl.pallas_call(kernel, name='conv_pair', out_shape=[jax.ShapeDtypeStruct(...]
where the time goes in v7:
time: 21.2 us; the launch traced here: 21.1 us
  Pallas kernels  21.1 us (100%)
    pallas_call x1, Pallas kernels, run_local(): pl.pallas_call(kernel, name='conv_pair', out_shape=[jax.ShapeDtypeStruct(...  20.1 us
    pallas_call x1, Pallas kernels, run_local(): pl.pallas_call(kernel_two, name='conv_last', out_shape=jax.ShapeDtypeStru...  1.03 us

profile of v7, /device:TPU:32, one launch (start us, length us, event | category | flops | bytes accessed | tf_op | source)
XLA Modules:
  0.0 21.1 jit_solution(11686282812102018613)
XLA Ops:
  0.0 0.0 copy-start
  0.0 20.1 %conv_pair.1 = (f32[8,14,8,256]{3,2,1,0:T(8,128)S(1)}, bf16[10,144,256]{2,1,0:T(8,128)(2,1)S(1)}, bf16[10,128,256]{2,1,0:T(8,128)(2,1)S(1)}, bf16[3,3,256,256]{3,2,1,0:T(8,128)(2,1)S(1)}) custom-call(bf16[8,128,128]{2,1,0:T(8,128)(2,1)} %bitcast.6, bf16[3,3,256]{2,1,0:T(4,128)(2,1)} %bitcast.7, f32[1,256]{1,0:T(1,128)} %bitcast.8, ...), custom_call_target="tpu_custom_call" | custom-call | tf_op jit(solution)/shard_map/conv_pair/pallas_call | solution.py:299
  20.1 0.0 copy-done
  20.1 1.0 %conv_last.1 = f32[8,16,8,256]{3,2,1,0:T(8,128)} custom-call(f32[8,14,8,256]{3,2,1,0:T(8,128)S(1)} %get-tuple-element.9.out_a, bf16[10,144,256]{2,1,0:T(8,128)(2,1)S(1)} %get-tuple-element.10.ys0, bf16[10,128,256]{2,1,0:T(8,128)(2,1)S(1)} %get-tuple-element.11.ys8, bf16[3,3,256,256]{3,2,1,0:T(8,128)(2,1)S(1)} %get-tuple-element.12.w2_mat, f32[1,256]{1,0:T(1,128)S(1)} %bitcast.5), custom_call_target="tpu_custom_call" | custom-call | tf_op jit(solution)/shard_map/conv_last/pallas_call | solution.py:336
Async XLA Ops:
  0.0 20.1 %copy-start = (f32[256]{0:T(256)S(1)}, f32[256]{0:T(256)}, u32[]{:S(2)}) copy-start(f32[256]{0:T(256)} %param.9) | copy-start | bytes 3076

commit v8 on v7

--- a/solution.py
+++ b/solution.py
@@ -29,12 +29,12 @@
 
 
 GREET_ORDER = greet_order()
-LATER_Z = ((0, 6, 14, 11), (100, 100, 108, 105))
-LATER_Y = ((20, 6, 0, 10), (20, 8, 0, 12))
-LATER_X = ((-3, 0, -1, -2), (0.0, 0.31000000000000005, 0.30000000000000004, 0.1))
-LATER_CORE = -0.01
+LATER_Z = ((0, 3, 17, 11), (100, 100, 108, 105))
+LATER_Y = ((20, 6, 0, 12), (17, 8, 0, 12))
+LATER_X = ((-6, 0, -1, -2), (0.0, 0.31, 0.3, 0.1))
+LATER_CORE = 0.01
 MIX = (0, 1, 1, 1, 1, 1)
-EARLY = (1,)
+EARLY = (1, 2)
 
 
 def send_order():

time: 21.2 us -> 21 us (level)
  the two profiles are of different devices: /device:TPU:32 before, /device:TPU:38 now
where the time goes in v8:
time: 21 us; the launch traced here: 20.8 us
  Pallas kernels  20.8 us (99%)
    pallas_call x1, Pallas kernels, run_local(): pl.pallas_call(kernel, name='conv_pair', out_shape=[jax.ShapeDtypeStruct(...  19.8 us
    pallas_call x1, Pallas kernels, run_local(): pl.pallas_call(kernel_two, name='conv_last', out_shape=jax.ShapeDtypeStru...  1.03 us

profile of v8, /device:TPU:38, one launch (start us, length us, event | category | flops | bytes accessed | tf_op | source)
XLA Modules:
  0.0 20.8 jit_solution(18329212345890891750)
XLA Ops:
  0.0 0.0 copy-start
  0.0 19.8 %conv_pair.1 = (f32[8,14,8,256]{3,2,1,0:T(8,128)S(1)}, bf16[10,144,256]{2,1,0:T(8,128)(2,1)S(1)}, bf16[10,128,256]{2,1,0:T(8,128)(2,1)S(1)}, bf16[3,3,256,256]{3,2,1,0:T(8,128)(2,1)S(1)}) custom-call(bf16[8,128,128]{2,1,0:T(8,128)(2,1)} %bitcast.6, bf16[3,3,256]{2,1,0:T(4,128)(2,1)} %bitcast.7, f32[1,256]{1,0:T(1,128)} %bitcast.8, ...), custom_call_target="tpu_custom_call" | custom-call | tf_op jit(solution)/shard_map/conv_pair/pallas_call | solution.py:299
  19.8 0.0 copy-done
  19.8 1.0 %conv_last.1 = f32[8,16,8,256]{3,2,1,0:T(8,128)} custom-call(f32[8,14,8,256]{3,2,1,0:T(8,128)S(1)} %get-tuple-element.9.out_a, bf16[10,144,256]{2,1,0:T(8,128)(2,1)S(1)} %get-tuple-element.10.ys0, bf16[10,128,256]{2,1,0:T(8,128)(2,1)S(1)} %get-tuple-element.11.ys8, bf16[3,3,256,256]{3,2,1,0:T(8,128)(2,1)S(1)} %get-tuple-element.12.w2_mat, f32[1,256]{1,0:T(1,128)S(1)} %bitcast.5), custom_call_target="tpu_custom_call" | custom-call | tf_op jit(solution)/shard_map/conv_last/pallas_call | solution.py:336
Async XLA Ops:
  0.0 19.8 %copy-start = (f32[256]{0:T(256)S(1)}, f32[256]{0:T(256)}, u32[]{:S(2)}) copy-start(f32[256]{0:T(256)} %param.9) | copy-start | bytes 3076

commit v9 on v8

--- a/solution.py
+++ b/solution.py
@@ -29,10 +29,10 @@
 
 
 GREET_ORDER = greet_order()
-LATER_Z = ((0, 3, 17, 11), (100, 100, 108, 105))
+LATER_Z = ((0, 3, 17, 11), (100, 100, 109, 105))
 LATER_Y = ((20, 6, 0, 12), (17, 8, 0, 12))
 LATER_X = ((-6, 0, -1, -2), (0.0, 0.31, 0.3, 0.1))
-LATER_CORE = 0.01
+LATER_CORE = 0.5
 MIX = (0, 1, 1, 1, 1, 1)
 EARLY = (1, 2)
 

time: 21 us -> 20.8 us (level)
  the two profiles are of different devices: /device:TPU:38 before, /device:TPU:97 now
where the time goes in v9:
time: 20.8 us; the launch traced here: 20.7 us
  Pallas kernels  20.7 us (100%)
    pallas_call x1, Pallas kernels, run_local(): pl.pallas_call(kernel, name='conv_pair', out_shape=[jax.ShapeDtypeStruct(...  19.7 us
    pallas_call x1, Pallas kernels, run_local(): pl.pallas_call(kernel_two, name='conv_last', out_shape=jax.ShapeDtypeStru...  1.03 us

profile of v9, /device:TPU:97, one launch (start us, length us, event | category | flops | bytes accessed | tf_op | source)
XLA Modules:
  0.0 20.7 jit_solution(12654794505973508258)
XLA Ops:
  0.0 0.0 copy-start
  0.0 19.7 %conv_pair.1 = (f32[8,14,8,256]{3,2,1,0:T(8,128)S(1)}, bf16[10,144,256]{2,1,0:T(8,128)(2,1)S(1)}, bf16[10,128,256]{2,1,0:T(8,128)(2,1)S(1)}, bf16[3,3,256,256]{3,2,1,0:T(8,128)(2,1)S(1)}) custom-call(bf16[8,128,128]{2,1,0:T(8,128)(2,1)} %bitcast.6, bf16[3,3,256]{2,1,0:T(4,128)(2,1)} %bitcast.7, f32[1,256]{1,0:T(1,128)} %bitcast.8, ...), custom_call_target="tpu_custom_call" | custom-call | tf_op jit(solution)/shard_map/conv_pair/pallas_call | solution.py:299
  19.7 0.0 copy-done
  19.7 1.0 %conv_last.1 = f32[8,16,8,256]{3,2,1,0:T(8,128)} custom-call(f32[8,14,8,256]{3,2,1,0:T(8,128)S(1)} %get-tuple-element.9.out_a, bf16[10,144,256]{2,1,0:T(8,128)(2,1)S(1)} %get-tuple-element.10.ys0, bf16[10,128,256]{2,1,0:T(8,128)(2,1)S(1)} %get-tuple-element.11.ys8, bf16[3,3,256,256]{3,2,1,0:T(8,128)(2,1)S(1)} %get-tuple-element.12.w2_mat, f32[1,256]{1,0:T(1,128)S(1)} %bitcast.5), custom_call_target="tpu_custom_call" | custom-call | tf_op jit(solution)/shard_map/conv_last/pallas_call | solution.py:336
Async XLA Ops:
  0.0 19.7 %copy-start = (f32[256]{0:T(256)S(1)}, f32[256]{0:T(256)}, u32[]{:S(2)}) copy-start(f32[256]{0:T(256)} %param.9) | copy-start | bytes 3076

commit v10 on v9

--- a/solution.py
+++ b/solution.py
@@ -34,7 +34,7 @@
 LATER_X = ((-6, 0, -1, -2), (0.0, 0.31, 0.3, 0.1))
 LATER_CORE = 0.5
 MIX = (0, 1, 1, 1, 1, 1)
-EARLY = (1, 2)
+EARLY = (1, 2, 3)
 
 
 def send_order():

time: 20.8 us -> 21.1 us (1.014)
  the two profiles are of different devices: /device:TPU:97 before, /device:TPU:41 now
where the time goes in v10:
time: 21.1 us; the launch traced here: 21 us
  Pallas kernels  20.9 us (99%)
    pallas_call x1, Pallas kernels, run_local(): pl.pallas_call(kernel, name='conv_pair', out_shape=[jax.ShapeDtypeStruct(...  19.9 us
    pallas_call x1, Pallas kernels, run_local(): pl.pallas_call(kernel_two, name='conv_last', out_shape=jax.ShapeDtypeStru...  1.03 us

profile of v10, /device:TPU:41, one launch (start us, length us, event | category | flops | bytes accessed | tf_op | source)
XLA Modules:
  0.0 21.0 jit_solution(8739159973777333060)
XLA Ops:
  0.0 0.0 copy-start
  0.0 19.9 %conv_pair.1 = (f32[8,14,8,256]{3,2,1,0:T(8,128)S(1)}, bf16[10,144,256]{2,1,0:T(8,128)(2,1)S(1)}, bf16[10,128,256]{2,1,0:T(8,128)(2,1)S(1)}, bf16[3,3,256,256]{3,2,1,0:T(8,128)(2,1)S(1)}) custom-call(bf16[8,128,128]{2,1,0:T(8,128)(2,1)} %bitcast.6, bf16[3,3,256]{2,1,0:T(4,128)(2,1)} %bitcast.7, f32[1,256]{1,0:T(1,128)} %bitcast.8, ...), custom_call_target="tpu_custom_call" | custom-call | tf_op jit(solution)/shard_map/conv_pair/pallas_call | solution.py:299
  19.9 0.0 copy-done
  19.9 1.0 %conv_last.1 = f32[8,16,8,256]{3,2,1,0:T(8,128)} custom-call(f32[8,14,8,256]{3,2,1,0:T(8,128)S(1)} %get-tuple-element.9.out_a, bf16[10,144,256]{2,1,0:T(8,128)(2,1)S(1)} %get-tuple-element.10.ys0, bf16[10,128,256]{2,1,0:T(8,128)(2,1)S(1)} %get-tuple-element.11.ys8, bf16[3,3,256,256]{3,2,1,0:T(8,128)(2,1)S(1)} %get-tuple-element.12.w2_mat, f32[1,256]{1,0:T(1,128)S(1)} %bitcast.5), custom_call_target="tpu_custom_call" | custom-call | tf_op jit(solution)/shard_map/conv_last/pallas_call | solution.py:336
Async XLA Ops:
  0.0 19.9 %copy-start = (f32[256]{0:T(256)S(1)}, f32[256]{0:T(256)}, u32[]{:S(2)}) copy-start(f32[256]{0:T(256)} %param.9) | copy-start | bytes 3076

commit v11 on v9

--- a/solution.py
+++ b/solution.py
@@ -29,7 +29,7 @@
 
 
 GREET_ORDER = greet_order()
-LATER_Z = ((0, 3, 17, 11), (100, 100, 109, 105))
+LATER_Z = ((0, 3, 17, 11), (100, 100, 109, 104))
 LATER_Y = ((20, 6, 0, 12), (17, 8, 0, 12))
 LATER_X = ((-6, 0, -1, -2), (0.0, 0.31, 0.3, 0.1))
 LATER_CORE = 0.5

time: 20.8 us -> 20.9 us (level)
  the two profiles are of different devices: /device:TPU:97 before, /device:TPU:56 now
where the time goes in v11:
time: 20.9 us; the launch traced here: 20.8 us
  Pallas kernels  20.7 us (99%)
    pallas_call x1, Pallas kernels, run_local(): pl.pallas_call(kernel, name='conv_pair', out_shape=[jax.ShapeDtypeStruct(...  19.7 us
    pallas_call x1, Pallas kernels, run_local(): pl.pallas_call(kernel_two, name='conv_last', out_shape=jax.ShapeDtypeStru...  1.03 us

profile of v11, /device:TPU:56, one launch (start us, length us, event | category | flops | bytes accessed | tf_op | source)
XLA Modules:
  0.0 20.8 jit_solution(10160624975653819383)
XLA Ops:
  0.0 0.0 copy-start
  0.0 19.7 %conv_pair.1 = (f32[8,14,8,256]{3,2,1,0:T(8,128)S(1)}, bf16[10,144,256]{2,1,0:T(8,128)(2,1)S(1)}, bf16[10,128,256]{2,1,0:T(8,128)(2,1)S(1)}, bf16[3,3,256,256]{3,2,1,0:T(8,128)(2,1)S(1)}) custom-call(bf16[8,128,128]{2,1,0:T(8,128)(2,1)} %bitcast.6, bf16[3,3,256]{2,1,0:T(4,128)(2,1)} %bitcast.7, f32[1,256]{1,0:T(1,128)} %bitcast.8, ...), custom_call_target="tpu_custom_call" | custom-call | tf_op jit(solution)/shard_map/conv_pair/pallas_call | solution.py:299
  19.7 0.0 copy-done
  19.7 1.0 %conv_last.1 = f32[8,16,8,256]{3,2,1,0:T(8,128)} custom-call(f32[8,14,8,256]{3,2,1,0:T(8,128)S(1)} %get-tuple-element.9.out_a, bf16[10,144,256]{2,1,0:T(8,128)(2,1)S(1)} %get-tuple-element.10.ys0, bf16[10,128,256]{2,1,0:T(8,128)(2,1)S(1)} %get-tuple-element.11.ys8, bf16[3,3,256,256]{3,2,1,0:T(8,128)(2,1)S(1)} %get-tuple-element.12.w2_mat, f32[1,256]{1,0:T(1,128)S(1)} %bitcast.5), custom_call_target="tpu_custom_call" | custom-call | tf_op jit(solution)/shard_map/conv_last/pallas_call | solution.py:336
Async XLA Ops:
  0.0 19.7 %copy-start = (f32[256]{0:T(256)S(1)}, f32[256]{0:T(256)}, u32[]{:S(2)}) copy-start(f32[256]{0:T(256)} %param.9) | copy-start | bytes 3076
